TPU v7x, 32 devices: a whole 2x2x4 slice. The times are simulated.
32 devices in a mesh: gx: 4 (over z), gy: 2 (over x), gz: 4 (over y, core).
Axes of the slice: x: 2, y: 2, z: 4, core: 2. Of those that a mesh axis runs over, the one named last changes fastest.
Arguments:
- block_x: float32 [16, 24, 12, 512], P(None, 'gz', 'gy', 'gx')
- block_hx: float32 [16, 24, 12, 512], P(None, 'gz', 'gy', 'gx')
- block_p: float32 [16, 24, 12, 512], P(None, 'gz', 'gy', 'gx')
- block_hp: float32 [16, 24, 12, 512], P(None, 'gz', 'gy', 'gx')
- potential: float32 [24, 12, 512], P('gz', 'gy', 'gx'), may hold values from -2 to 2
- projectors: float32 [4, 2, 4, 8, 4, 256], P('gz', 'gy', 'gx'), may hold values from -0.75 to 0.75
- coupling: float32 [4, 2, 4, 8, 4, 4], P('gz', 'gy', 'gx'), may hold values from 0.25 to 1.25
- atom_count: int32 [4, 2, 4], P('gz', 'gy', 'gx'), may hold values from 0 to 8, as said below
- proj_count: int32 [4, 2, 4, 8], P('gz', 'gy', 'gx'), may hold values from 1 to 4
- offsets: int32 [3, 4, 2, 4, 8], P(None, 'gz', 'gy', 'gx'), may hold values from 0 to 127, as said below
- extents: int32 [3, 4, 2, 4, 8], P(None, 'gz', 'gy', 'gx'), may hold values from 2 to 16, as said below
Outputs:
- w_block: float32 [16, 24, 12, 512], P(None, 'gz', 'gy', 'gx')
- hw_block: float32 [16, 24, 12, 512], P(None, 'gz', 'gy', 'gx')
- gram: float32 [48, 48], replicated
- rayleigh: float32 [48, 48], replicated
Inputs may be any that keep to these rules, and one draw needn't show every extreme that they name: `atom_count`: slots at and above a domain's count are empty; some domain is full in every draw. The first proj_count projectors of a slot are used. `offsets`: components z, y, x are below 6, 6, 128. `extents`: components z, y, x are at most 4, 4, 16; some slot has the full box in every draw.
All inputs are finite; a program needn't handle non-finite values.
Results may differ from a plain program's by a relative error of at most 0.0003.
Values sent between devices are 32-bit elements; how exact they have to be, the bound alone decides.
A program may use at most 64 MiB of HBM per device.

v0:
```python
import functools

import jax
import jax.numpy as jnp
from jax import lax
from jax.experimental import pallas as pl
from jax.experimental.pallas import tpu as pltpu
from jax.sharding import PartitionSpec as P

BZ, BY, BX = 4, 4, 16
LAP_CENTER = -5369.0 / 1800.0
LAP_COEFFS = (12.0 / 7.0, -15.0 / 56.0, 10.0 / 189.0, -1.0 / 112.0, 2.0 / 1925.0, -1.0 / 16632.0)
MESH = pl.DeviceIdType.MESH
AXES = ("gz", "gy", "gx")
F32 = jnp.float32
BF16 = jnp.bfloat16
HP, HX, XX, PP, WW, HW = range(6)


def tiles_of(count):
    return -(-count // 8)


def kernel(
    sizes, groups, dims,
    off_ref, ext_ref, count_ref, proj_ref, d_ref, x_in, hx_in, p_in, hp_in, v_ref, beta_ref,
    w_ref, hw_ref, gram_ref, ray_ref, red1_ref,
    stack, zext, ybuf, zybuf, plow, phigh, xr, xl, frame, frame_x, halo_x,
    blo, bhi, pieces, nf, nh, spack, rz, ry, rzy, rx, wout,
    *rest,
):
    cz, cy, cx, slots, nproj, cols = dims
    nz, ny, nx = sizes
    n_red = len(groups)
    bufs = (rest[:n_red], rest[n_red : 2 * n_red])
    rest = rest[2 * n_red :]
    red_send, red_recv, halo_send, halo_recv, spill_send, spill_recv = rest[:6]
    load_sem, x_ref, hx_ref, p_ref, hp_ref = rest[6:]
    loads = []
    for i, (source, target) in enumerate(
        ((x_in, x_ref), (hx_in, hx_ref), (p_in, p_ref), (hp_in, hp_ref))
    ):
        loads.append(pltpu.make_async_copy(source, target, load_sem.at[i]))
        loads[-1].start()
    zi, yi, xi = (lax.axis_index(a) for a in AXES)
    size_of = dict(zip(AXES, sizes))
    here = dict(zip(AXES, (zi, yi, xi)))
    fz, fy = cz + BZ - 1, cy + BY - 1
    own = cz * cy
    lane = lax.broadcasted_iota(jnp.int32, (cols, 128), 1)

    def neighbour(dz, dy, dx):
        step = dict(zip(AXES, (dz, dy, dx)))
        return {a: lax.rem(here[a] + step[a] + size_of[a], size_of[a]) for a in AXES}

    def member(group, offset):
        total = 1
        index = 0
        for a in group:
            total *= size_of[a]
            index = index * size_of[a] + here[a]
        target = lax.rem(index + offset, total)
        device = {}
        for a in reversed(group):
            device[a] = lax.rem(target, size_of[a])
            target = target // size_of[a]
        return {a: device.get(a, here[a]) for a in AXES}, index, total

    octant = [(1, 0, 0), (0, 1, 0), (1, 1, 0), (0, 0, 1), (1, 0, 1), (0, 1, 1), (1, 1, 1)]
    barrier = pltpu.get_barrier_semaphore()
    greeted = 0
    for group in groups:
        total = member(group, 0)[2]
        for offset in range(1, total):
            pl.semaphore_signal(
                barrier, inc=1, device_id=member(group, offset)[0], device_id_type=MESH
            )
            greeted += 1
    for dz, dy, dx in octant:
        for sign in (1, -1):
            pl.semaphore_signal(
                barrier, inc=1, device_id=neighbour(sign * dz, sign * dy, sign * dx),
                device_id_type=MESH,
            )
            greeted += 1

    def split_store(kind, cell, value):
        high = value.astype(BF16)
        low = (value - high.astype(F32)).astype(BF16)
        start = cell * 128 if isinstance(cell, int) else pl.multiple_of(cell * 128, 128)
        stack[kind * 32 : kind * 32 + 32, pl.ds(start, 128)] = jnp.concatenate([high, low], 0)

    for load in loads:
        load.wait()

    @pl.loop(0, cz)
    def _(z):
        for y in range(cy):
            cell = z * cy + y
            split_store(HX, cell, hx_ref[cell])
            split_store(HP, cell, hp_ref[cell])
            split_store(XX, cell, x_ref[cell])
            split_store(PP, cell, p_ref[cell])

    def products(left, right_from, right_to, count=1):
        m = lax.dot_general(
            stack[left * 32 : (left + count) * 32, :],
            stack[right_from * 32 : right_to * 32, :],
            (((1,), (1,)), ((), ())),
            preferred_element_type=F32,
        )
        parts = [m[32 * i : 32 * i + cols] + m[32 * i + cols : 32 * i + 32] for i in range(count)]
        return parts if count > 1 else parts[0]

    def reduced(which, payload):
        base = which * sum(member(g, 0)[2] for g in groups)
        for phase, group in enumerate(groups):
            buf = bufs[which][phase]
            _, index, total = member(group, 0)
            buf[index] = payload
            if phase == 0 and which == 0:
                pl.semaphore_wait(barrier, greeted)
            copies = []
            for offset in range(1, total):
                copies.append(
                    pltpu.make_async_remote_copy(
                        src_ref=buf.at[index],
                        dst_ref=buf.at[index],
                        send_sem=red_send.at[base + offset],
                        recv_sem=red_recv.at[base + offset],
                        device_id=member(group, offset)[0],
                        device_id_type=MESH,
                    )
                )
                copies[-1].start()
            base += total
            yield None
            for copy in copies:
                copy.wait()
            payload = buf[0]
            for slot in range(1, total):
                payload = payload + buf[slot]
        yield payload

    def finish(steps):
        out = None
        for out in steps:
            pass
        return out

    hx_row, x_row, p_row = products(HX, HP, WW, 3)
    first = jnp.where((lane >= 32) & (lane < 64), pltpu.roll(hx_row, 96, 1), x_row)

    def paired(upper, lower):
        upper = upper + pltpu.roll(upper, 112, 1)
        lower = lower + pltpu.roll(lower, 112, 1)
        return jnp.where(lane % 32 < 16, upper, pltpu.roll(lower, 16, 1))

    reduction = reduced(0, paired(first, p_row))
    next(reduction)

    per_slot = BZ * BY * nproj
    lane_p = lax.broadcasted_iota(jnp.int32, (nproj, 128), 1)
    row_p = lax.broadcasted_iota(jnp.int32, (nproj, 128), 0)
    in_tile = 128 // BX
    for s in range(slots):
        ox = off_ref[2, 0, 0, 0, s]
        along = lax.rem(lane_p - ox + 128, 128)
        along = jnp.where(row_p < proj_ref[0, s], along, 128)
        low_side = lane_p >= ox
        live = s < count_ref[0, 0]
        for a in range(BZ):
            for b in range(BY):
                used = live & (a < ext_ref[0, 0, 0, 0, s]) & (b < ext_ref[1, 0, 0, 0, s])
                limit = jnp.where(used, jnp.minimum(ext_ref[2, 0, 0, 0, s], BX), 0)
                box = a * BY + b
                part = beta_ref[s, :, (box // in_tile) * 128 : (box // in_tile) * 128 + 128]
                part = pltpu.roll(part, lax.rem(ox + 128 - BX * (box % in_tile), 128), 1)
                part = jnp.where(along < limit, part, 0.0)
                row = s * per_slot + box * nproj
                blo[row : row + nproj, :] = jnp.where(low_side, part, 0.0)
                bhi[row : row + nproj, :] = jnp.where(low_side, 0.0, part)
    rim_y = BY + 2
    rim = (BZ + 2) * rim_y

    @pl.loop(0, slots)
    def _(s):
        for i in range(rim):
            if i < rim_y or i >= rim - rim_y or i % rim_y in (0, rim_y - 1):
                pieces[s * rim + i] = jnp.zeros(pieces.shape[1:], F32)

    sums1 = finish(reduction)
    red1_ref[...] = sums1
    matrix = jnp.concatenate([pltpu.roll(sums1, 64, 1), pltpu.roll(sums1, 96, 1)], 0)
    lane2 = lax.broadcasted_iota(jnp.int32, (2 * cols, 128), 1)
    matrix = jnp.where(lane2 < cols, matrix, 0.0)
    for k in range(0, cols, 2):
        row0, row1 = matrix[k : k + 1, :], matrix[k + 1 : k + 2, :]
        col0, col1 = matrix[:, k : k + 1], matrix[:, k + 1 : k + 2]
        a, b = matrix[k : k + 1, k : k + 1], matrix[k : k + 1, k + 1 : k + 2]
        c, d = matrix[k + 1 : k + 2, k : k + 1], matrix[k + 1 : k + 2, k + 1 : k + 2]
        ratio = c / a
        schur = d - ratio * b
        new1 = (col1 - col0 * (b / a)) / schur
        new0 = col0 / a - new1 * ratio
        rest_of = matrix - new0 * row0 - new1 * row1
        matrix = jnp.where(lane2 == k, new0, jnp.where(lane2 == k + 1, new1, rest_of))
    theta_t = matrix[cols:, :]
    theta_cols = [jnp.broadcast_to(theta_t[:, k : k + 1], (cols, 128)) for k in range(cols)]

    @pl.loop(0, cz)
    def _(z):
        for y in range(cy):
            cell = z * cy + y
            xs = x_ref[cell]
            value = hx_ref[cell]
            for k in range(cols):
                value = value - theta_cols[k] * xs[k : k + 1, :]
            vv = v_ref[z, y : y + 1, :]
            value = value / (1.0 + vv * vv)
            zext[cz + z, y] = value
            w_ref[cell] = value
            split_store(WW, cell, value)

    for q in range(tiles_of(own)):
        low = jnp.zeros((cols, 128), F32)
        high = low
        for j in range(min(8, own - 8 * q)):
            tile = zext[cz + (8 * q + j) // cy, (8 * q + j) % cy]
            keep = (lane >= 16 * j) & (lane < 16 * j + 16)
            low = jnp.where(keep, pltpu.roll(tile, 16 * j, 1) if j else tile, low)
            high = jnp.where(keep, pltpu.roll(tile, (16 * j + 16) % 128, 1) if j < 7 else tile, high)
        plow[q] = low
        phigh[q] = high

    two_y = ny == 2
    more_z, more_y = fz - cz, fy - cy
    z_tiles = tiles_of(more_z * cy)
    corner_tiles = tiles_of((more_z - 1) * cy + more_y)

    def some(ref, z, dz, y, dy):
        return ref.at[pl.ds(z, dz), pl.ds(y, dy)]

    def layers(target, base, z, dz, y, dy, where):
        return some(zext, cz + z, dz, y, dy), some(target, base + z, dz, y, dy), where

    early = [
        (some(zext, cz, more_z, 0, more_y), zybuf, (-1, -1, 0)),
        (plow.at[pl.ds(0, corner_tiles)], xr.at[3, pl.ds(0, corner_tiles)], (-1, -1, -1)),
        (plow, xr.at[2], (0, -1, -1)),
        (plow.at[pl.ds(0, z_tiles)], xr.at[1, pl.ds(0, z_tiles)], (-1, 0, -1)),
        (plow, xr.at[0], (0, 0, -1)),
        layers(ybuf.at[1], 0, 0, cz, 0, more_y, (0, -1, 0)),
        layers(zext, 2 * cz, 0, more_z, 0, cy, (-1, 0, 0)),
    ]
    late = [
        (phigh, xl, (0, 0, 1)),
        layers(ybuf.at[1], 0, 0, cz, more_y, cy - more_y, (0, -1, 0)),
        layers(zext, 2 * cz, more_z, cz - more_z, 0, cy, (-1, 0, 0)),
        layers(zext, 0, 0, cz, 0, cy, (1, 0, 0)),
    ]
    if not two_y:
        late.append(layers(ybuf.at[0], 0, 0, cz, 0, cy, (0, 1, 0)))

    def launch(sends, send_sem, recv_sem, first=0):
        copies = []
        for i, (source, target, where) in enumerate(sends, start=first):
            copies.append(
                pltpu.make_async_remote_copy(
                    src_ref=source,
                    dst_ref=target,
                    send_sem=send_sem.at[i],
                    recv_sem=recv_sem.at[i],
                    device_id=neighbour(*where),
                    device_id_type=MESH,
                )
            )
            copies[-1].start()
        return copies

    copies = launch(early, halo_send, halo_recv)
    late_copies = launch(late, halo_send, halo_recv, len(early))
    w_row = products(WW, HP, WW)
    w_row2 = products(WW, XX, HW)
    for copy in copies:
        copy.wait()

    below_y = 1 if two_y else 0
    for z in range(fz):
        for y in range(fy):
            up_z, up_y = z >= cz, y >= cy
            local = (z - cz * up_z) * cy + (y - cy * up_y)
            if up_z and up_y:
                tile = zybuf[z - cz, y - cy]
            elif up_z:
                tile = zext[cz + z, y]
            elif up_y:
                tile = ybuf[1, z, y - cy]
            else:
                tile = zext[cz + z, y]
            frame[z * fy + y] = tile
            shift = (128 - 16 * (local % 8)) % 128
            tile = xr[up_z + 2 * up_y, local // 8]
            tile = pltpu.roll(tile, shift, 1) if shift else tile
            frame_x[z * fy + y] = tile

    @pl.loop(0, slots)
    def _(s):
        oz, oy = off_ref[0, 0, 0, 0, s], off_ref[1, 0, 0, 0, s]
        sums = [jnp.zeros((cols, 128), F32) for _ in range(nproj)]
        for a in range(BZ):
            for b in range(BY):
                at = (oz + a) * fy + oy + b
                tile, tile_x = frame[at], frame_x[at]
                base = s * per_slot + (a * BY + b) * nproj
                for q in range(nproj):
                    sums[q] = sums[q] + tile * blo[pl.ds(base + q, 1), :]
                    sums[q] = sums[q] + jnp.where(
                        lane < 16, tile_x * bhi[pl.ds(base + q, 1), :], 0.0
                    )
        overlaps = [jnp.broadcast_to(jnp.sum(v, axis=1, keepdims=True), (cols, 128)) for v in sums]
        outs = []
        dm = d_ref[0, 0, 0, s]
        for p in range(nproj):
            value = overlaps[p] * dm[p : p + 1, p : p + 1]
            for q in range(nproj):
                if q != p:
                    value = value + overlaps[q] * (0.5 * (dm[p : p + 1, q : q + 1] + dm[q : q + 1, p : p + 1]))
            outs.append(value)
        for a in range(BZ):
            for b in range(BY):
                base = s * per_slot + (a * BY + b) * nproj
                low = outs[0] * blo[pl.ds(base, 1), :]
                high = outs[0] * bhi[pl.ds(base, 1), :]
                for p in range(1, nproj):
                    low = low + outs[p] * blo[pl.ds(base + p, 1), :]
                    high = high + outs[p] * bhi[pl.ds(base + p, 1), :]
                place = s * rim + (a + 1) * rim_y + b + 1
                pieces[place, 0] = low
                pieces[place, 1] = high

    @pl.loop(0, fz)
    def _(z):
        starts = []
        for s in range(slots):
            a = jnp.minimum(jnp.maximum(z - off_ref[0, 0, 0, 0, s], -1), BZ) + 1
            starts.append(s * rim + a * rim_y)
        for y in range(fy):
            low = jnp.zeros((cols, 128), F32)
            high = low
            for s in range(slots):
                b = jnp.minimum(jnp.maximum(y - off_ref[1, 0, 0, 0, s], -1), BY) + 1
                low = low + pieces[starts[s] + b, 0]
                high = high + pieces[starts[s] + b, 1]
            nf[z, y] = low
            nh[z, y] = high

    spans = []
    filled = 0
    for up_z in (0, 1):
        for up_y in (0, 1):
            cells = [
                (z, y)
                for z in (range(cz, fz) if up_z else range(cz))
                for y in (range(cy, fy) if up_y else range(cy))
            ]
            spans.append((filled, up_z, up_y, cells))
            for q in range(tiles_of(len(cells))):
                tile = jnp.zeros((cols, 128), F32)
                for j, (z, y) in enumerate(cells[8 * q : 8 * q + 8]):
                    keep = (lane >= 16 * j) & (lane < 16 * j + 16)
                    value = nh[z, y]
                    tile = jnp.where(keep, pltpu.roll(value, 16 * j, 1) if j else value, tile)
                spack[filled + q] = tile
            filled += tiles_of(len(cells))
    sends = [
        (nf.at[pl.ds(cz, more_z), pl.ds(0, cy)], rz, (1, 0, 0)),
        (nf.at[pl.ds(0, cz), pl.ds(cy, more_y)], ry, (0, 1, 0)),
        (nf.at[pl.ds(cz, more_z), pl.ds(cy, more_y)], rzy, (1, 1, 0)),
    ]
    for begin, up_z, up_y, cells in spans:
        part = pl.ds(begin, tiles_of(len(cells)))
        sends.append((spack.at[part], rx.at[part], (up_z, up_y, 1)))
    copies = launch(sends, spill_send, spill_recv)

    for copy in late_copies:
        copy.wait()
    for cell in range(own):
        turn = (112 - 16 * (cell % 8)) % 128
        left = xl[cell // 8]
        left = pltpu.roll(left, turn, 1) if turn else left
        halo_x[cell] = jnp.where(lane < 64, frame_x[cell // cy * fy + cell % cy], left)

    @pl.loop(0, cz)
    def _(z):
        for y in range(cy):
            cell = z * cy + y
            centre = zext[cz + z, y]
            edge = halo_x[cell]
            vv = v_ref[z, y : y + 1, :]
            total = centre * (vv - 1.5 * LAP_CENTER)
            for k, weight in enumerate(LAP_COEFFS, start=1):
                beside = zext[cz + z + k, y] + zext[cz + z - k, y]
                for target in (y + k, y - k):
                    if target >= cy:
                        beside = beside + ybuf[1, z, target - cy]
                    elif target < 0:
                        beside = beside + ybuf[below_y, z, target + cy]
                    else:
                        beside = beside + zext[cz + z, target]
                beside = beside + pltpu.roll(jnp.where(lane < k, edge, centre), 128 - k, 1)
                beside = beside + pltpu.roll(jnp.where(lane >= 128 - k, edge, centre), k, 1)
                total = total - 0.5 * weight * beside
            hw_ref[cell] = total + nf[z, y]

    for copy in copies:
        copy.wait()
    for z in range(cz):
        for y in range(cy):
            cell = z * cy + y
            value = hw_ref[cell]
            if z < more_z:
                value = value + rz[z, y]
            if y < more_y:
                value = value + ry[z, y]
            if z < more_z and y < more_y:
                value = value + rzy[z, y]
            extra = None
            for begin, up_z, up_y, cells in spans:
                where = (z + cz * up_z, y + cy * up_y)
                if where in cells:
                    index = cells.index(where)
                    tile = rx[begin + index // 8]
                    shift = (128 - 16 * (index % 8)) % 128
                    tile = pltpu.roll(tile, shift, 1) if shift else tile
                    extra = tile if extra is None else extra + tile
            value = value + jnp.where(lane < 16, extra, 0.0)
            hw_ref[cell] = value
            split_store(HW, cell, value)

    hw_row = products(HW, XX, HW + 1)
    second = jnp.where(lane < 96, hw_row, pltpu.roll(w_row2_pad(w_row2), 32, 1))
    sums2 = finish(reduced(1, paired(w_row, second)))
    weight = 1.0 / (own * cx * nz * ny * nx)
    sums1 = red1_ref[...]
    rows = jnp.concatenate([sums1, pltpu.roll(sums1, 112, 1), sums2, pltpu.roll(sums2, 112, 1)], 0)
    rows = rows * weight
    turned = jnp.transpose(jnp.concatenate([rows, jnp.zeros_like(rows)], 0))

    def direct(row, group, target):
        return rows[16 * row : 16 * row + 16, :], 32 * group, target

    def flipped(row, group, target):
        return turned[32 * group : 32 * group + 16, :], 16 * row, target

    def laid(parts):
        total = None
        for tile, begin, target in parts:
            shift = (16 * target - begin) % 128
            tile = pltpu.roll(tile, shift, 1) if shift else tile
            tile = jnp.where((lane >= 16 * target) & (lane < 16 * target + 16), tile, 0.0)
            total = tile if total is None else total + tile
        return total

    gram = [
        [direct(0, 2, 0), flipped(2, 2, 1), direct(0, 3, 2)],
        [direct(2, 2, 0), direct(3, 3, 1), direct(2, 3, 2)],
        [direct(1, 2, 0), flipped(2, 3, 1), direct(1, 3, 2)],
    ]
    rayleigh = [
        [flipped(0, 1, 0), flipped(3, 0, 1), direct(0, 0, 2)],
        [direct(2, 1, 0), flipped(3, 2, 1), direct(2, 0, 2)],
        [direct(1, 1, 0), flipped(3, 1, 1), direct(1, 0, 2)],
    ]
    for i in range(3):
        gram_ref[16 * i : 16 * i + 16, :] = laid(gram[i])[:, :48]
        ray_ref[16 * i : 16 * i + 16, :] = laid(rayleigh[i])[:, :48]


def put_out(*refs):
    half = len(refs) // 2
    for source, target in zip(refs[:half], refs[half:]):
        target[...] = source[...]


def w_row2_pad(row):
    return jnp.concatenate([row, jnp.zeros((row.shape[0], 128 - row.shape[1]), row.dtype)], 1)


def per_device(
    sizes,
    block_x, block_hx, block_p, block_hp, potential, projectors, coupling,
    atom_count, proj_count, offsets, extents,
):
    cols, cz, cy, cx = block_x.shape
    slots, nproj = projectors.shape[-3], projectors.shape[-2]
    nz, ny, nx = sizes
    own = cz * cy
    fz, fy = cz + BZ - 1, cy + BY - 1
    turned = [
        jnp.transpose(b, (1, 2, 0, 3)).reshape(own, cols, cx)
        for b in (block_x, block_hx, block_p, block_hp)
    ]
    groups = (("gz", "gy"), ("gx",)) if nz * ny <= 16 else (("gz",), ("gy",), ("gx",))
    size_of = dict(zip(AXES, sizes))
    totals = []
    for group in groups:
        total = 1
        for a in group:
            total *= size_of[a]
        totals.append(total)
    tile = (cols, 128)
    more_z, more_y = fz - cz, fy - cy
    packed = sum(
        tiles_of(zc * yc) for zc in (cz, more_z) for yc in (cy, more_y)
    )
    per_slot = BZ * BY * nproj
    scratch = [
        pltpu.VMEM((cols, 128), F32),
        pltpu.VMEM((192, own * 128), BF16),
        pltpu.VMEM((3 * cz, cy) + tile, F32),
        pltpu.VMEM((2, cz, cy) + tile, F32),
        pltpu.VMEM((BZ - 1, BY - 1) + tile, F32),
        pltpu.VMEM((tiles_of(own),) + tile, F32),
        pltpu.VMEM((tiles_of(own),) + tile, F32),
        pltpu.VMEM((4, tiles_of(own)) + tile, F32),
        pltpu.VMEM((tiles_of(own),) + tile, F32),
        pltpu.VMEM((fz * fy,) + tile, F32),
        pltpu.VMEM((fz * fy,) + tile, F32),
        pltpu.VMEM((own,) + tile, F32),
        pltpu.VMEM((slots * per_slot, 128), F32),
        pltpu.VMEM((slots * per_slot, 128), F32),
        pltpu.VMEM((slots * (BZ + 2) * (BY + 2), 2) + tile, F32),
        pltpu.VMEM((fz, fy) + tile, F32),
        pltpu.VMEM((fz, fy) + tile, F32),
        pltpu.VMEM((packed,) + tile, F32),
        pltpu.VMEM((more_z, cy) + tile, F32),
        pltpu.VMEM((cz, more_y) + tile, F32),
        pltpu.VMEM((more_z, more_y) + tile, F32),
        pltpu.VMEM((packed,) + tile, F32),
        pltpu.VMEM((8, 128), F32),
    ]
    scratch += [pltpu.VMEM((t, cols, 128), F32) for t in totals] * 2
    scratch += [
        pltpu.SemaphoreType.DMA((2 * sum(totals),)),
        pltpu.SemaphoreType.DMA((2 * sum(totals),)),
        pltpu.SemaphoreType.DMA((12,)),
        pltpu.SemaphoreType.DMA((12,)),
        pltpu.SemaphoreType.DMA((7,)),
        pltpu.SemaphoreType.DMA((7,)),
        pltpu.SemaphoreType.DMA((4,)),
    ]
    scratch += [pltpu.VMEM((own,) + tile, F32)] * 4
    vmem = pl.BlockSpec(memory_space=pltpu.VMEM)
    smem = pl.BlockSpec(memory_space=pltpu.SMEM)
    w, hw, gram, rayleigh = pl.pallas_call(
        functools.partial(kernel, sizes, groups, (cz, cy, cx, slots, nproj, cols)),
        out_shape=(
            jax.ShapeDtypeStruct((own,) + tile, F32),
            jax.ShapeDtypeStruct((own,) + tile, F32),
            jax.ShapeDtypeStruct((3 * cols, 3 * cols), F32),
            jax.ShapeDtypeStruct((3 * cols, 3 * cols), F32),
        ),
        in_specs=[smem] * 4 + [vmem] + [pl.BlockSpec(memory_space=pl.ANY)] * 4 + [vmem] * 2,
        out_specs=(vmem,) * 4,
        scratch_shapes=scratch,
        compiler_params=pltpu.CompilerParams(collective_id=0, has_side_effects=True),
    )(
        offsets, extents, atom_count[0], proj_count[0, 0], coupling,
        *turned, potential, projectors[0, 0, 0],
    )
    w, hw, gram, rayleigh = pl.pallas_call(
        put_out,
        out_shape=tuple(jax.ShapeDtypeStruct(b.shape, F32) for b in (w, hw, gram, rayleigh)),
        in_specs=[vmem] * 4,
        out_specs=(vmem,) * 4,
    )(w, hw, gram, rayleigh)
    w, hw = (jnp.transpose(b.reshape(cz, cy, cols, cx), (2, 0, 1, 3)) for b in (w, hw))
    return (w, hw, gram, rayleigh)


def solution(mesh):
    sizes = tuple(mesh.shape[a] for a in AXES)
    in_specs = (
        P(None, "gz", "gy", "gx"),
        P(None, "gz", "gy", "gx"),
        P(None, "gz", "gy", "gx"),
        P(None, "gz", "gy", "gx"),
        P("gz", "gy", "gx"),
        P("gz", "gy", "gx", None, None, None),
        P("gz", "gy", "gx", None, None, None),
        P("gz", "gy", "gx"),
        P("gz", "gy", "gx", None),
        P(None, "gz", "gy", "gx", None),
        P(None, "gz", "gy", "gx", None),
    )
    out_specs = (P(None, "gz", "gy", "gx"), P(None, "gz", "gy", "gx"), P(), P())
    return jax.shard_map(
        functools.partial(per_device, sizes),
        mesh=mesh, in_specs=in_specs, out_specs=out_specs, check_vma=False,
    )
```

profile of v0, /device:TPU:0, one launch (start us, length us, event | category | flops | bytes accessed | tf_op | source)
XLA Modules:
  0.0 49.5 jit_solution(12919950887355030190)
XLA Ops:
  0.6 0.0 copy-start
  1.3 0.0 copy-done
  1.3 0.7 %copy.15.d_ref = f32[1,1,1,8,4,4]{5,4,3,2,1,0:T(4,128)} copy(f32[1,1,1,8,4,4]{3,5,4,2,1,0:T(4,128)S(1)} %copy-done) | data formatting | bytes 1024 | tf_op args[6]
  2.0 45.6 %shard_map.138 = (f32[36,16,128]{2,1,0:T(8,128)}, f32[36,16,128]{2,1,0:T(8,128)}, f32[48,48]{1,0:T(8,128)}, f32[48,48]{1,0:T(8,128)}) custom-call(s32[3,1,1,1,8]{4,3,2,1,0:T(1,128)} %off_ref.1, s32[3,1,1,1,8]{4,3,2,1,0:T(1,128)} %ext_ref.1, s32[1,1]{1,0:T(1,128)} %bitcast.21.count_ref, s32[1,8]{1,0:T(1,128)} %bitcast.27, f32[1,1,1,8,4,4]{5,4,3,2,1,0:T(4,128)} %copy.15.d_ref, ...), custom_call_target="tpu_custom_call" | custom-call | tf_op jit(solution)/shard_map/pallas_call | solution.py:556
  47.6 1.9 %shard_map.139 = (f32[36,16,128]{2,1,0:T(8,128)}, f32[36,16,128]{2,1,0:T(8,128)}, f32[48,48]{1,0:T(8,128)}, f32[48,48]{1,0:T(8,128)}) custom-call(f32[36,16,128]{2,1,0:T(8,128)} %get-tuple-element.12.refs_0_, f32[36,16,128]{2,1,0:T(8,128)} %get-tuple-element.13.refs_1_, f32[48,48]{1,0:T(8,128)} %get-tuple-element.14.refs_2_, f32[48,48]{1,0:T(8,128)} %get-tuple-element.15.refs_3_), custom_call_target="tpu_custom_call" | custom-call | tf_op jit(solution)/shard_map/pallas_call | solution.py:572
Async XLA Ops:
  0.6 0.7 %copy-start = (f32[1,1,1,8,4,4]{3,5,4,2,1,0:T(4,128)S(1)}, f32[1,1,1,8,4,4]{3,5,4,2,1,0:T(4,128)}, u32[]{:S(2)}) copy-start(f32[1,1,1,8,4,4]{3,5,4,2,1,0:T(4,128)} %param.17) | copy-start | bytes 1540
where the time goes:
time: 49.8 us; the launch traced here: 49.5 us
  Pallas kernels  47.4 us (95%)
  between operations  1.31 us (3%)
  local copies, waits for them, and re-layouts  0.73 us (1%)
    pallas_call x1, Pallas kernels, per_device(): pl.pallas_call(functools.partial(kernel, sizes, groups, (cz, cy, cx, slot...  45.6 us
    pallas_call x1, Pallas kernels, per_device(): pl.pallas_call(put_out, out_shape=tuple((jax.ShapeDtypeStruct(b.shape, F3...  1.89 us

commit v1 on v0

--- a/solution.py
+++ b/solution.py
@@ -11,6 +11,7 @@
 LAP_CENTER = -5369.0 / 1800.0
 LAP_COEFFS = (12.0 / 7.0, -15.0 / 56.0, 10.0 / 189.0, -1.0 / 112.0, 2.0 / 1925.0, -1.0 / 16632.0)
 MESH = pl.DeviceIdType.MESH
+VMEM_LIMIT = (63 << 20) - (64 << 10)
 AXES = ("gz", "gy", "gx")
 F32 = jnp.float32
 BF16 = jnp.bfloat16
@@ -21,10 +22,65 @@
     return -(-count // 8)
 
 
+def solved(packed, cols, acol):
+    shape = (8, 128)
+
+    def spread(lane_at):
+        return jnp.broadcast_to(packed[:, lane_at : lane_at + 1], shape)
+
+    for j in range(cols):
+        if j < 8:
+            acol[j, 0:8] = spread(2 * cols + j)
+        acol[j, 8:16] = spread(3 * cols + j)
+    a = {}
+    for j in range(cols):
+        for i in range(j, cols):
+            a[i, j] = jnp.broadcast_to(acol[j, i : i + 1, :], shape)
+    scale = [lax.rsqrt(a[i, i]) for i in range(cols)]
+    for i, j in a:
+        a[i, j] = a[i, j] * scale[i] * scale[j]
+    right = [
+        [spread(half * cols + k) * scale[k] for half in range(2)] for k in range(cols)
+    ]
+    low = {}
+    inverse = []
+    for k in range(0, cols, 2):
+        p, q, r = a[k, k], a[k + 1, k], a[k + 1, k + 1]
+        det = 1.0 / (p * r - q * q)
+        p, q, r = r * det, -q * det, p * det
+        inverse.append((p, q, r))
+        for i in range(k + 2, cols):
+            low[i, k] = a[i, k] * p + a[i, k + 1] * q
+            low[i, k + 1] = a[i, k] * q + a[i, k + 1] * r
+            for j in range(k + 2, i + 1):
+                a[i, j] = a[i, j] - (low[i, k] * a[j, k] + low[i, k + 1] * a[j, k + 1])
+            right[i] = [
+                right[i][h] - (low[i, k] * right[k][h] + low[i, k + 1] * right[k + 1][h])
+                for h in range(2)
+            ]
+    out = [None] * cols
+    for k in range(cols - 2, -1, -2):
+        p, q, r = inverse[k // 2]
+        halves = []
+        for h in range(2):
+            first = right[k][h] * p + right[k + 1][h] * q
+            second = right[k][h] * q + right[k + 1][h] * r
+            for i in range(cols - 1, k + 1, -1):
+                first = first - low[i, k] * out[i][h]
+                second = second - low[i, k + 1] * out[i][h]
+            halves.append((first, second))
+        out[k] = [halves[0][0], halves[1][0]]
+        out[k + 1] = [halves[0][1], halves[1][1]]
+    return [
+        jnp.concatenate([out[k][0] * scale[k], out[k][1] * scale[k]], 0) for k in range(cols)
+    ]
+
+
 def kernel(
     sizes, groups, dims,
-    off_ref, ext_ref, count_ref, proj_ref, d_ref, x_in, hx_in, p_in, hp_in, v_ref, beta_ref,
-    w_ref, hw_ref, gram_ref, ray_ref, red1_ref,
+    off_ref, ext_ref, count_ref, proj_ref, d_in, x_in, hx_in, p_in, hp_in, v_in, beta_in,
+    w_out, hw_out, gram_out, ray_out, red1_ref, w_ref, hw_ref, gram_ref, ray_ref,
+    acol, dtab, d_ref, v_ref, beta_ref,
     stack, zext, ybuf, zybuf, plow, phigh, xr, xl, frame, frame_x, halo_x,
     blo, bhi, pieces, nf, nh, spack, rz, ry, rzy, rx, wout,
     *rest,
@@ -32,13 +88,16 @@
     cz, cy, cx, slots, nproj, cols = dims
     nz, ny, nx = sizes
     n_red = len(groups)
-    bufs = (rest[:n_red], rest[n_red : 2 * n_red])
-    rest = rest[2 * n_red :]
+    bufs = (rest[:n_red], rest[n_red : 2 * n_red], rest[2 * n_red : 3 * n_red])
+    rest = rest[3 * n_red :]
     red_send, red_recv, halo_send, halo_recv, spill_send, spill_recv = rest[:6]
-    load_sem, x_ref, hx_ref, p_ref, hp_ref = rest[6:]
+    load_sem, out_sem, x_ref, hx_ref, p_ref, hp_ref = rest[6:]
     loads = []
     for i, (source, target) in enumerate(
-        ((x_in, x_ref), (hx_in, hx_ref), (p_in, p_ref), (hp_in, hp_ref))
+        (
+            (x_in, x_ref), (hx_in, hx_ref), (v_in, v_ref), (beta_in, beta_ref),
+            (p_in, p_ref), (hp_in, hp_ref), (d_in, d_ref),
+        )
     ):
         loads.append(pltpu.make_async_copy(source, target, load_sem.at[i]))
         loads[-1].start()
@@ -90,17 +149,17 @@
         start = cell * 128 if isinstance(cell, int) else pl.multiple_of(cell * 128, 128)
         stack[kind * 32 : kind * 32 + 32, pl.ds(start, 128)] = jnp.concatenate([high, low], 0)
 
-    for load in loads:
+    def split_all(*kinds):
+        @pl.loop(0, cz)
+        def _(z):
+            for y in range(cy):
+                cell = z * cy + y
+                for kind, ref in kinds:
+                    split_store(kind, cell, ref[cell])
+
+    for load in loads[:2]:
         load.wait()
-
-    @pl.loop(0, cz)
-    def _(z):
-        for y in range(cy):
-            cell = z * cy + y
-            split_store(HX, cell, hx_ref[cell])
-            split_store(HP, cell, hp_ref[cell])
-            split_store(XX, cell, x_ref[cell])
-            split_store(PP, cell, p_ref[cell])
+    split_all((HX, hx_ref), (XX, x_ref))
 
     def products(left, right_from, right_to, count=1):
         m = lax.dot_general(
@@ -118,7 +177,7 @@
             buf = bufs[which][phase]
             _, index, total = member(group, 0)
             buf[index] = payload
-            if phase == 0 and which == 0:
+            if phase == 0 and which == 2:
                 pl.semaphore_wait(barrier, greeted)
             copies = []
             for offset in range(1, total):
@@ -148,6 +207,27 @@
             pass
         return out
 
+    both = lax.dot_general(
+        stack[HX * 32 : XX * 32 + 32, :], stack[XX * 32 : XX * 32 + 32, :],
+        (((1,), (1,)), ((), ())), preferred_element_type=F32,
+    )
+    both = jnp.concatenate([both, jnp.zeros((64, 96), F32)], 1)
+    turn_hx = both[:cols] + both[cols:32]
+    corr = both[32 : 32 + cols] + both[32 + cols :]
+    narrow = lax.broadcasted_iota(jnp.int32, (8, 128), 1)
+
+    def merged(tile):
+        return tile + pltpu.roll(tile, 128 - cols, 1)
+
+    payload0 = jnp.where(narrow < cols, merged(turn_hx[:8]), 0.0)
+    for at, tile in ((1, turn_hx[8:]), (2, corr[:8]), (3, corr[8:])):
+        moved = pltpu.roll(merged(tile), at * cols, 1)
+        payload0 = jnp.where((narrow >= at * cols) & (narrow < at * cols + cols), moved, payload0)
+    solving = reduced(2, payload0)
+    next(solving)
+    for load in loads[2:]:
+        load.wait()
+    split_all((HP, hp_ref), (PP, p_ref))
     hx_row, x_row, p_row = products(HX, HP, WW, 3)
     first = jnp.where((lane >= 32) & (lane < 64), pltpu.roll(hx_row, 96, 1), x_row)
 
@@ -157,7 +237,6 @@
         return jnp.where(lane % 32 < 16, upper, pltpu.roll(lower, 16, 1))
 
     reduction = reduced(0, paired(first, p_row))
-    next(reduction)
 
     per_slot = BZ * BY * nproj
     lane_p = lax.broadcasted_iota(jnp.int32, (nproj, 128), 1)
@@ -168,7 +247,7 @@
         along = lax.rem(lane_p - ox + 128, 128)
         along = jnp.where(row_p < proj_ref[0, s], along, 128)
         low_side = lane_p >= ox
-        live = s < count_ref[0, 0]
+        live = s < count_ref[0, 0, 0]
         for a in range(BZ):
             for b in range(BY):
                 used = live & (a < ext_ref[0, 0, 0, 0, s]) & (b < ext_ref[1, 0, 0, 0, s])
@@ -180,6 +259,11 @@
                 row = s * per_slot + box * nproj
                 blo[row : row + nproj, :] = jnp.where(low_side, part, 0.0)
                 bhi[row : row + nproj, :] = jnp.where(low_side, 0.0, part)
+    for p in range(nproj):
+        for s in range(slots):
+            dtab[s, p * nproj : p * nproj + nproj, :] = jnp.broadcast_to(
+                d_ref[p, :, s : s + 1], (nproj, 128)
+            )
     rim_y = BY + 2
     rim = (BZ + 2) * rim_y
 
@@ -189,24 +273,12 @@
             if i < rim_y or i >= rim - rim_y or i % rim_y in (0, rim_y - 1):
                 pieces[s * rim + i] = jnp.zeros(pieces.shape[1:], F32)
 
-    sums1 = finish(reduction)
-    red1_ref[...] = sums1
-    matrix = jnp.concatenate([pltpu.roll(sums1, 64, 1), pltpu.roll(sums1, 96, 1)], 0)
-    lane2 = lax.broadcasted_iota(jnp.int32, (2 * cols, 128), 1)
-    matrix = jnp.where(lane2 < cols, matrix, 0.0)
-    for k in range(0, cols, 2):
-        row0, row1 = matrix[k : k + 1, :], matrix[k + 1 : k + 2, :]
-        col0, col1 = matrix[:, k : k + 1], matrix[:, k + 1 : k + 2]
-        a, b = matrix[k : k + 1, k : k + 1], matrix[k : k + 1, k + 1 : k + 2]
-        c, d = matrix[k + 1 : k + 2, k : k + 1], matrix[k + 1 : k + 2, k + 1 : k + 2]
-        ratio = c / a
-        schur = d - ratio * b
-        new1 = (col1 - col0 * (b / a)) / schur
-        new0 = col0 / a - new1 * ratio
-        rest_of = matrix - new0 * row0 - new1 * row1
-        matrix = jnp.where(lane2 == k, new0, jnp.where(lane2 == k + 1, new1, rest_of))
-    theta_t = matrix[cols:, :]
-    theta_cols = [jnp.broadcast_to(theta_t[:, k : k + 1], (cols, 128)) for k in range(cols)]
+    next(solving)
+    next(reduction)
+    sums0 = finish(solving)
+    next(reduction)
+    sums0 = solved(sums0, cols, acol)
+    theta_cols = sums0
 
     @pl.loop(0, cz)
     def _(z):
@@ -217,7 +289,7 @@
             for k in range(cols):
                 value = value - theta_cols[k] * xs[k : k + 1, :]
             vv = v_ref[z, y : y + 1, :]
-            value = value / (1.0 + vv * vv)
+            value = value * (1.0 / (1.0 + vv * vv))
             zext[cz + z, y] = value
             w_ref[cell] = value
             split_store(WW, cell, value)
@@ -280,8 +352,16 @@
 
     copies = launch(early, halo_send, halo_recv)
     late_copies = launch(late, halo_send, halo_recv, len(early))
+    outs = [
+        pltpu.make_async_copy(source, target, out_sem.at[i])
+        for i, (source, target) in enumerate(
+            ((w_ref, w_out), (hw_ref, hw_out), (gram_ref, gram_out), (ray_ref, ray_out))
+        )
+    ]
+    outs[0].start()
     w_row = products(WW, HP, WW)
     w_row2 = products(WW, XX, HW)
+    red1_ref[...] = finish(reduction)
     for copy in copies:
         copy.wait()
 
@@ -320,12 +400,16 @@
                     )
         overlaps = [jnp.broadcast_to(jnp.sum(v, axis=1, keepdims=True), (cols, 128)) for v in sums]
         outs = []
-        dm = d_ref[0, 0, 0, s]
+        dm = {}
         for p in range(nproj):
-            value = overlaps[p] * dm[p : p + 1, p : p + 1]
+            for q in range(nproj):
+                at = p * nproj + q
+                dm[p, q] = dtab[s, at : at + 1, :]
+        for p in range(nproj):
+            value = overlaps[p] * dm[p, p]
             for q in range(nproj):
                 if q != p:
-                    value = value + overlaps[q] * (0.5 * (dm[p : p + 1, q : q + 1] + dm[q : q + 1, p : p + 1]))
+                    value = value + overlaps[q] * (0.5 * (dm[p, q] + dm[q, p]))
             outs.append(value)
         for a in range(BZ):
             for b in range(BY):
@@ -438,6 +522,7 @@
             hw_ref[cell] = value
             split_store(HW, cell, value)
 
+    outs[1].start()
     hw_row = products(HW, XX, HW + 1)
     second = jnp.where(lane < 96, hw_row, pltpu.roll(w_row2_pad(w_row2), 32, 1))
     sums2 = finish(reduced(1, paired(w_row, second)))
@@ -475,12 +560,23 @@
     for i in range(3):
         gram_ref[16 * i : 16 * i + 16, :] = laid(gram[i])[:, :48]
         ray_ref[16 * i : 16 * i + 16, :] = laid(rayleigh[i])[:, :48]
+    for out in outs[2:]:
+        out.start()
+    for out in outs:
+        out.wait()
 
 
 def put_out(*refs):
+    sems = refs[-1]
     half = len(refs) // 2
-    for source, target in zip(refs[:half], refs[half:]):
-        target[...] = source[...]
+    copies = [
+        pltpu.make_async_copy(source, target, sems.at[i])
+        for i, (source, target) in enumerate(zip(refs[:half], refs[half : 2 * half]))
+    ]
+    for copy in copies:
+        copy.start()
+    for copy in copies:
+        copy.wait()
 
 
 def w_row2_pad(row):
@@ -517,6 +613,15 @@
     per_slot = BZ * BY * nproj
     scratch = [
         pltpu.VMEM((cols, 128), F32),
+        pltpu.VMEM((own,) + tile, F32),
+        pltpu.VMEM((own,) + tile, F32),
+        pltpu.VMEM((3 * cols, 3 * cols), F32),
+        pltpu.VMEM((3 * cols, 3 * cols), F32),
+        pltpu.VMEM((cols, cols, 128), F32),
+        pltpu.VMEM((slots, nproj * nproj, 128), F32),
+        pltpu.VMEM((nproj, nproj, slots), F32),
+        pltpu.VMEM(potential.shape, F32),
+        pltpu.VMEM(projectors.shape[3:], F32),
         pltpu.VMEM((192, own * 128), BF16),
         pltpu.VMEM((3 * cz, cy) + tile, F32),
         pltpu.VMEM((2, cz, cy) + tile, F32),
@@ -541,11 +646,13 @@
         pltpu.VMEM((8, 128), F32),
     ]
     scratch += [pltpu.VMEM((t, cols, 128), F32) for t in totals] * 2
+    scratch += [pltpu.VMEM((t, 8, 128), F32) for t in totals]
     scratch += [
-        pltpu.SemaphoreType.DMA((2 * sum(totals),)),
-        pltpu.SemaphoreType.DMA((2 * sum(totals),)),
+        pltpu.SemaphoreType.DMA((3 * sum(totals),)),
+        pltpu.SemaphoreType.DMA((3 * sum(totals),)),
         pltpu.SemaphoreType.DMA((12,)),
         pltpu.SemaphoreType.DMA((12,)),
+        pltpu.SemaphoreType.DMA((7,)),
         pltpu.SemaphoreType.DMA((7,)),
         pltpu.SemaphoreType.DMA((7,)),
         pltpu.SemaphoreType.DMA((4,)),
@@ -556,24 +663,29 @@
     w, hw, gram, rayleigh = pl.pallas_call(
         functools.partial(kernel, sizes, groups, (cz, cy, cx, slots, nproj, cols)),
         out_shape=(
-            jax.ShapeDtypeStruct((own,) + tile, F32),
-            jax.ShapeDtypeStruct((own,) + tile, F32),
-            jax.ShapeDtypeStruct((3 * cols, 3 * cols), F32),
-            jax.ShapeDtypeStruct((3 * cols, 3 * cols), F32),
+            pltpu.VMEM((own,) + tile, F32),
+            pltpu.VMEM((own,) + tile, F32),
+            pltpu.VMEM((3 * cols, 3 * cols), F32),
+            pltpu.VMEM((3 * cols, 3 * cols), F32),
         ),
-        in_specs=[smem] * 4 + [vmem] + [pl.BlockSpec(memory_space=pl.ANY)] * 4 + [vmem] * 2,
-        out_specs=(vmem,) * 4,
+        in_specs=[smem] * 4 + [pl.BlockSpec(memory_space=pltpu.HBM)] * 7,
+        out_specs=(pl.BlockSpec(memory_space=pl.ANY),) * 4,
         scratch_shapes=scratch,
-        compiler_params=pltpu.CompilerParams(collective_id=0, has_side_effects=True),
+        compiler_params=pltpu.CompilerParams(
+            collective_id=0, has_side_effects=True, vmem_limit_bytes=VMEM_LIMIT
+        ),
     )(
-        offsets, extents, atom_count[0], proj_count[0, 0], coupling,
+        offsets, extents, atom_count, proj_count[0, 0],
+        jnp.transpose(coupling[0, 0, 0], (1, 2, 0)),
         *turned, potential, projectors[0, 0, 0],
     )
     w, hw, gram, rayleigh = pl.pallas_call(
         put_out,
         out_shape=tuple(jax.ShapeDtypeStruct(b.shape, F32) for b in (w, hw, gram, rayleigh)),
         in_specs=[vmem] * 4,
-        out_specs=(vmem,) * 4,
+        out_specs=(pl.BlockSpec(memory_space=pl.ANY),) * 4,
+        scratch_shapes=[pltpu.SemaphoreType.DMA((4,))],
+        compiler_params=pltpu.CompilerParams(vmem_limit_bytes=4 << 20),
     )(w, hw, gram, rayleigh)
     w, hw = (jnp.transpose(b.reshape(cz, cy, cols, cx), (2, 0, 1, 3)) for b in (w, hw))
     return (w, hw, gram, rayleigh)

time: 49.8 us -> 44.9 us (0.902)
  Pallas kernels: 47.4 us -> 43.4 us
  local copies, waits for them, and re-layouts: 0.73 us -> 0 us
    pallas_call x1, Pallas kernels: 45.6 us -> 42.6 us  [per_device(): pl.pallas_call(functools.partial(kernel, sizes, groups, (cz, cy, cx, slot...]
    pallas_call x1, Pallas kernels: 1.89 us -> 0.85 us  [per_device(): pl.pallas_call(put_out, out_shape=tuple((jax.ShapeDtypeStruct(b.shape, F3...]
    unnamed x3 -> x0, local copies, waits for them, and re-layouts: 0.73 us -> none
where the time goes in v1:
time: 44.9 us; the launch traced here: 44.7 us
  Pallas kernels  43.4 us (97%)
  between operations  1.29 us (3%)
    pallas_call x1, Pallas kernels, per_device(): pl.pallas_call(functools.partial(kernel, sizes, groups, (cz, cy, cx, slot...  42.6 us

profile of v1, /device:TPU:0, one launch (start us, length us, event | category | flops | bytes accessed | tf_op | source)
XLA Modules:
  0.0 44.7 jit_solution(5899749709886119668)
XLA Ops:
  1.3 42.6 %shard_map.138 = (f32[36,16,128]{2,1,0:T(8,128)S(1)}, f32[36,16,128]{2,1,0:T(8,128)S(1)}, f32[48,48]{1,0:T(8,128)S(1)}, f32[48,48]{1,0:T(8,128)S(1)}) custom-call(s32[3,1,1,1,8]{4,3,2,1,0:T(1,128)} %off_ref.1, s32[3,1,1,1,8]{4,3,2,1,0:T(1,128)} %ext_ref.1, s32[1,1,1]{2,1,0:T(1,128)S(6)} %copy.15.count_ref, s32[1,8]{1,0:T(1,128)} %bitcast.29, ...), custom_call_target="tpu_custom_call" | custom-call | tf_op jit(solution)/shard_map/pallas_call | solution.py:663
  43.9 0.9 %shard_map.139 = (f32[36,16,128]{2,1,0:T(8,128)}, f32[36,16,128]{2,1,0:T(8,128)}, f32[48,48]{1,0:T(8,128)}, f32[48,48]{1,0:T(8,128)}) custom-call(f32[36,16,128]{2,1,0:T(8,128)S(1)} %get-tuple-element.12.refs_0_, f32[36,16,128]{2,1,0:T(8,128)S(1)} %get-tuple-element.13.refs_1_, f32[48,48]{1,0:T(8,128)S(1)} %get-tuple-element.14.refs_2_, ...), custom_call_target="tpu_custom_call" | custom-call | tf_op jit(solution)/shard_map/pallas_call | solution.py:682

commit v2 on v1

v2 whole, which is shorter than its diff:
```python
import functools

import jax
import jax.numpy as jnp
from jax import lax
from jax.experimental import pallas as pl
from jax.experimental.pallas import tpu as pltpu
from jax.sharding import PartitionSpec as P

BZ, BY, BX = 4, 4, 16
LAP_CENTER = -5369.0 / 1800.0
LAP_COEFFS = (12.0 / 7.0, -15.0 / 56.0, 10.0 / 189.0, -1.0 / 112.0, 2.0 / 1925.0, -1.0 / 16632.0)
MESH = pl.DeviceIdType.MESH
VMEM_LIMIT = (63 << 20) - (64 << 10)
AXES = ("gz", "gy", "gx")
F32 = jnp.float32
BF16 = jnp.bfloat16
HP, HX, XX, PP, WW, HW = range(6)


def tiles_of(count):
    return -(-count // 8)


def solved(packed, cols, acol):
    shape = (8, 128)

    def spread(lane_at):
        return jnp.broadcast_to(packed[:, lane_at : lane_at + 1], shape)

    for j in range(cols):
        if j < 8:
            acol[j, 0:8] = spread(2 * cols + j)
        acol[j, 8:16] = spread(3 * cols + j)
    a = {}
    for j in range(cols):
        for i in range(j, cols):
            a[i, j] = jnp.broadcast_to(acol[j, i : i + 1, :], shape)
    scale = [lax.rsqrt(a[i, i]) for i in range(cols)]
    for i, j in a:
        a[i, j] = a[i, j] * scale[i] * scale[j]
    right = [
        [spread(half * cols + k) * scale[k] for half in range(2)] for k in range(cols)
    ]
    low = {}
    inverse = []
    for k in range(0, cols, 2):
        p, q, r = a[k, k], a[k + 1, k], a[k + 1, k + 1]
        det = 1.0 / (p * r - q * q)
        p, q, r = r * det, -q * det, p * det
        inverse.append((p, q, r))
        for i in range(k + 2, cols):
            low[i, k] = a[i, k] * p + a[i, k + 1] * q
            low[i, k + 1] = a[i, k] * q + a[i, k + 1] * r
            for j in range(k + 2, i + 1):
                a[i, j] = a[i, j] - (low[i, k] * a[j, k] + low[i, k + 1] * a[j, k + 1])
            right[i] = [
                right[i][h] - (low[i, k] * right[k][h] + low[i, k + 1] * right[k + 1][h])
                for h in range(2)
            ]
    out = [None] * cols
    for k in range(cols - 2, -1, -2):
        p, q, r = inverse[k // 2]
        halves = []
        for h in range(2):
            first = right[k][h] * p + right[k + 1][h] * q
            second = right[k][h] * q + right[k + 1][h] * r
            for i in range(cols - 1, k + 1, -1):
                first = first - low[i, k] * out[i][h]
                second = second - low[i, k + 1] * out[i][h]
            halves.append((first, second))
        out[k] = [halves[0][0], halves[1][0]]
        out[k + 1] = [halves[0][1], halves[1][1]]
    return [
        jnp.concatenate([out[k][0] * scale[k], out[k][1] * scale[k]], 0) for k in range(cols)
    ]


def kernel(
    sizes, groups, dims,
    off_ref, ext_ref, count_ref, proj_ref, d_in, x_in, hx_in, p_in, hp_in, v_in, beta_in,
    w_out, hw_out, gram_out, ray_out, red1_ref, w_ref, hw_ref, gram_ref, ray_ref,
    acol, d_ref, v_ref, beta_ref,
    stack, zext, ybuf, plow, phigh, xr, xl, edges, inner, nf,
    shared, offs, lines, bnear, bfar, parts4, parts_in,
    *rest,
):
    cz, cy, cx, slots, nproj, cols = dims
    nz, ny, nx = sizes
    n_red = len(groups)
    bufs = (rest[:n_red], rest[n_red : 2 * n_red], rest[2 * n_red : 3 * n_red])
    rest = rest[3 * n_red :]
    red_send, red_recv, halo_send, halo_recv, atom_send, atom_recv, part_sem = rest[:7]
    load_sem, out_sem, x_ref, hx_ref, p_ref, hp_ref = rest[7:]
    loads = []
    for i, (source, target) in enumerate(
        (
            (x_in, x_ref), (hx_in, hx_ref), (v_in, v_ref), (beta_in, beta_ref),
            (p_in, p_ref), (hp_in, hp_ref), (d_in, d_ref),
        )
    ):
        loads.append(pltpu.make_async_copy(source, target, load_sem.at[i]))
        loads[-1].start()
    zi, yi, xi = (lax.axis_index(a) for a in AXES)
    size_of = dict(zip(AXES, sizes))
    here = dict(zip(AXES, (zi, yi, xi)))
    more_z, more_y = BZ - 1, BY - 1
    own = cz * cy
    lane = lax.broadcasted_iota(jnp.int32, (cols, 128), 1)

    def neighbour(dz, dy, dx):
        step = dict(zip(AXES, (dz, dy, dx)))
        return {a: lax.rem(here[a] + step[a] + size_of[a], size_of[a]) for a in AXES}

    def member(group, offset):
        total = 1
        index = 0
        for a in group:
            total *= size_of[a]
            index = index * size_of[a] + here[a]
        target = lax.rem(index + offset, total)
        device = {}
        for a in reversed(group):
            device[a] = lax.rem(target, size_of[a])
            target = target // size_of[a]
        return {a: device.get(a, here[a]) for a in AXES}, index, total

    octant = [(o // 4, o // 2 % 2, o % 2) for o in range(8)]
    around = [
        (dz, dy, dx)
        for dx in (-1, 0, 1) for dz in (-1, 0, 1) for dy in (-1, 0, 1)
        if (dz, dy, dx) != (0, 0, 0)
    ]
    barrier = pltpu.get_barrier_semaphore()
    greeted = 0
    for group in groups:
        total = member(group, 0)[2]
        for offset in range(1, total):
            pl.semaphore_signal(
                barrier, inc=1, device_id=member(group, offset)[0], device_id_type=MESH
            )
            greeted += 1
    for where in around:
        pl.semaphore_signal(
            barrier, inc=1, device_id=neighbour(*where), device_id_type=MESH
        )
        greeted += 1

    def split_store(kind, cell, value):
        high = value.astype(BF16)
        low = (value - high.astype(F32)).astype(BF16)
        start = cell * 128 if isinstance(cell, int) else pl.multiple_of(cell * 128, 128)
        stack[kind * 32 : kind * 32 + 32, pl.ds(start, 128)] = jnp.concatenate([high, low], 0)

    def split_all(*kinds):
        @pl.loop(0, cz)
        def _(z):
            for y in range(cy):
                cell = z * cy + y
                for kind, ref in kinds:
                    split_store(kind, cell, ref[cell])

    for load in loads[:2]:
        load.wait()
    split_all((HX, hx_ref), (XX, x_ref))

    def products(left, right_from, right_to, count=1):
        m = lax.dot_general(
            stack[left * 32 : (left + count) * 32, :],
            stack[right_from * 32 : right_to * 32, :],
            (((1,), (1,)), ((), ())),
            preferred_element_type=F32,
        )
        parts = [m[32 * i : 32 * i + cols] + m[32 * i + cols : 32 * i + 32] for i in range(count)]
        return parts if count > 1 else parts[0]

    def reduced(which, payload):
        for phase, group in enumerate(groups):
            buf = bufs[which][phase]
            _, index, total = member(group, 0)
            send_sem, recv_sem = (sem.at[which * n_red + phase] for sem in (red_send, red_recv))
            buf[index] = payload
            if phase == 0 and which == 2:
                pl.semaphore_wait(barrier, greeted)
            for offset in range(1, total):
                pltpu.make_async_remote_copy(
                    src_ref=buf.at[index],
                    dst_ref=buf.at[index],
                    send_sem=send_sem,
                    recv_sem=recv_sem,
                    device_id=member(group, offset)[0],
                    device_id_type=MESH,
                ).start()
            yield None
            most = buf.at[pl.ds(0, total - 1)]
            for sem in (recv_sem, send_sem):
                pltpu.make_async_copy(most, most, sem).wait()
            payload = buf[0]
            for slot in range(1, total):
                payload = payload + buf[slot]
        yield payload

    def finish(steps):
        out = None
        for out in steps:
            pass
        return out

    both = lax.dot_general(
        stack[HX * 32 : XX * 32 + 32, :], stack[XX * 32 : XX * 32 + 32, :],
        (((1,), (1,)), ((), ())), preferred_element_type=F32,
    )
    both = jnp.concatenate([both, jnp.zeros((64, 96), F32)], 1)
    turn_hx = both[:cols] + both[cols:32]
    corr = both[32 : 32 + cols] + both[32 + cols :]
    narrow = lax.broadcasted_iota(jnp.int32, (8, 128), 1)

    def merged(tile):
        return tile + pltpu.roll(tile, 128 - cols, 1)

    payload0 = jnp.where(narrow < cols, merged(turn_hx[:8]), 0.0)
    for at, tile in ((1, turn_hx[8:]), (2, corr[:8]), (3, corr[8:])):
        moved = pltpu.roll(merged(tile), at * cols, 1)
        payload0 = jnp.where((narrow >= at * cols) & (narrow < at * cols + cols), moved, payload0)
    solving = reduced(2, payload0)
    next(solving)
    for load in loads[2:]:
        load.wait()
    rows = slots * nproj
    pairs = rows // 8
    box_lane = lax.broadcasted_iota(jnp.int32, (nproj, BZ * BY * BX), 1)
    box_row = lax.broadcasted_iota(jnp.int32, (nproj, BZ * BY * BX), 0)
    box_a, box_b, box_c = box_lane // (BY * BX), box_lane // BX % BY, box_lane % BX
    for s in range(slots):
        kept = jnp.where(s < count_ref[0, 0, 0], proj_ref[0, s], 0)
        inside = (
            (box_row < kept)
            & (box_a < ext_ref[0, 0, 0, 0, s])
            & (box_b < ext_ref[1, 0, 0, 0, s])
            & (box_c < ext_ref[2, 0, 0, 0, s])
        )
        at = s * nproj
        shared[0, at // 8, at % 8 : at % 8 + nproj, :] = jnp.where(inside, beta_ref[s], 0.0)
    lane1 = lax.broadcasted_iota(jnp.int32, (1, 128), 1)
    lane16 = lax.broadcasted_iota(jnp.int32, (nproj, 128), 1)
    slot_at = lane16 % 64 // 16 * (8 // nproj) + lane16 % 8 // nproj
    table = []
    for p in range(nproj):
        mirrored = jnp.concatenate([d_ref[q, p : p + 1, :] for q in range(nproj)], 0)
        sym = 0.5 * (d_ref[p] + mirrored)
        spread = jnp.zeros((nproj, 128), F32)
        for s in range(slots):
            value = jnp.broadcast_to(sym[:, s : s + 1], (nproj, 128))
            spread = jnp.where(slot_at == s, value, spread)
        table.append(spread)
    for d in range(-nproj + 1, nproj):
        row = jnp.zeros((1, 128), F32)
        for p in range(max(0, -d), min(nproj, nproj - d)):
            row = jnp.where(lane1 % nproj == p, table[p][p + d : p + d + 1, :], row)
        shared[0, pairs, d + nproj - 1 : d + nproj, 0:128] = row
    atom_copies = {}
    for o in (4, 2, 1, 6, 5, 3, 7):
        atom_copies[o] = [
            pltpu.make_async_remote_copy(
                src_ref=source,
                dst_ref=target,
                send_sem=atom_send.at[2 * (o - 1) + i],
                recv_sem=atom_recv.at[2 * (o - 1) + i],
                device_id=neighbour(*octant[o]),
                device_id_type=MESH,
            )
            for i, (source, target) in enumerate(
                ((off_ref, offs.at[o - 1]), (shared.at[0], shared.at[o]))
            )
        ]
        for copy in atom_copies[o]:
            copy.start()
    split_all((HP, hp_ref), (PP, p_ref))
    hx_row, x_row, p_row = products(HX, HP, WW, 3)
    first = jnp.where((lane >= 32) & (lane < 64), pltpu.roll(hx_row, 96, 1), x_row)

    def paired(upper, lower):
        upper = upper + pltpu.roll(upper, 112, 1)
        lower = lower + pltpu.roll(lower, 112, 1)
        return jnp.where(lane % 32 < 16, upper, pltpu.roll(lower, 16, 1))

    reduction = reduced(0, paired(first, p_row))

    lane8 = lax.broadcasted_iota(jnp.int32, (8, 128), 1)
    row8 = lax.broadcasted_iota(jnp.int32, (8, 128), 0)
    in_tile = 128 // BX
    width = BY + cy - 1
    ahead = cy - 1
    nothing = ahead + slots * BZ * width + ahead
    blank = jnp.zeros((16, 128), BF16)
    blank_line = jnp.zeros((8, 128), F32)

    @pl.loop(0, slots * BZ)
    def _(block):
        for b in range(BY, width):
            lines[ahead + block * width + b] = blank_line

    for at in [*range(ahead), *range(nothing - ahead, nothing + width)]:
        lines[at] = blank_line

    def build(o):
        dz, dy, dx = octant[o]

        def expand(pair):
            tiles = shared[o, pair]
            for half in range(8 // nproj):
                s = pair * (8 // nproj) + half
                ox = offset(2, s)
                along = (lane8 - ox + 128) & 127
                side = lane8 < ox if dx else lane8 >= ox
                keep = (along < BX) & side & (row8 // nproj == half)
                for k in range(in_tile):
                    shift = (ox + 128 - BX * k) & 127
                    for at in range(k, BZ * BY, in_tile):
                        part = tiles[:, at // in_tile * 128 : at // in_tile * 128 + 128]
                        part = jnp.where(keep, pltpu.roll(part, shift, 1), 0.0)
                        lines[ahead + (s * BZ + at // BY) * width + at % BY] = part

        def offset(axis, s):
            return off_ref[axis, 0, 0, 0, s] if o == 0 else offs[o - 1, axis, 0, 0, 0, s]

        for pair in range(pairs):
            expand(pair)

        target = bfar if dz else bnear
        top = o % 4 * 64
        ys = more_y if dy else cy

        @pl.loop(0, more_z if dz else cz)
        def _(z):
            starts = []
            for s in range(slots):
                a = z + dz * cz - offset(0, s)
                ok = (a >= 0) & (a < BZ)
                start = jnp.where(ok, ahead + (s * BZ + a) * width - offset(1, s), nothing - offset(1, s))
                starts.append(start)
            for y in range(cy):
                column = pl.ds(pl.multiple_of((z * cy + y) * 128, 128), 128)
                for pair in range(pairs):
                    at = top + pair * 16
                    if y >= ys:
                        target[at : at + 16, column] = blank
                        continue
                    total = None
                    for half in range(8 // nproj):
                        start = starts[pair * (8 // nproj) + half] + (y + dy * cy)
                        part = lines[start]
                        total = part if total is None else total + part
                    high = total.astype(BF16)
                    low = (total - high.astype(F32)).astype(BF16)
                    target[at : at + 16, column] = jnp.concatenate([high, low], 0)

    for z in range(cz):
        for y in range(cy):
            inner[z, y] = jnp.zeros((cols, 128), F32)
            inner[2 * cz + z, y] = jnp.zeros((cols, 128), F32)
    build(0)
    next(solving)
    next(reduction)
    for o in (4, 1, 2, 5, 6, 3, 7):
        for copy in atom_copies[o]:
            copy.wait()
        build(o)
    sums0 = finish(solving)
    next(reduction)
    sums0 = solved(sums0, cols, acol)
    theta_cols = sums0

    @pl.loop(0, cz)
    def _(z):
        for y in range(cy):
            cell = z * cy + y
            xs = x_ref[cell]
            value = hx_ref[cell]
            for k in range(cols):
                value = value - theta_cols[k] * xs[k : k + 1, :]
            vv = v_ref[z, y : y + 1, :]
            value = value * (1.0 / (1.0 + vv * vv))
            zext[cz + z, y] = value
            inner[cz + z, y] = value
            w_ref[cell] = value
            split_store(WW, cell, value)

    two_y = ny == 2
    split = cz // 2

    def some(ref, z, dz, y, dy):
        return ref.at[pl.ds(z, dz), pl.ds(y, dy)]

    def layers(target, base, z, dz, where):
        return some(zext, cz + z, dz, 0, cy), some(target, base + z, dz, 0, cy), where

    def bulk(z, dz):
        sends = [
            layers(zext, 2 * cz, z, dz, (-1, 0, 0)),
            layers(zext, 0, z, dz, (1, 0, 0)),
            layers(ybuf.at[1], 0, z, dz, (0, -1, 0)),
        ]
        if not two_y:
            sends.append(layers(ybuf.at[0], 0, z, dz, (0, 1, 0)))
        return sends

    early = bulk(0, split)
    late = bulk(split, cz - split)

    def launch(sends, send_sem, recv_sem, first=0):
        copies = []
        for i, (source, target, where) in enumerate(sends, start=first):
            copies.append(
                pltpu.make_async_remote_copy(
                    src_ref=source,
                    dst_ref=target,
                    send_sem=send_sem.at[i],
                    recv_sem=recv_sem.at[i],
                    device_id=neighbour(*where),
                    device_id_type=MESH,
                )
            )
            copies[-1].start()
        return copies

    copies = launch(early, halo_send, halo_recv)
    outs = [
        pltpu.make_async_copy(source, target, out_sem.at[i])
        for i, (source, target) in enumerate(
            ((w_ref, w_out), (hw_ref, hw_out), (gram_ref, gram_out), (ray_ref, ray_out))
        )
    ]
    outs[0].start()
    for q in range(tiles_of(own)):
        low = jnp.zeros((cols, 128), F32)
        high = low
        for j in range(min(8, own - 8 * q)):
            tile = zext[cz + (8 * q + j) // cy, (8 * q + j) % cy]
            keep = (lane >= 16 * j) & (lane < 16 * j + 16)
            low = jnp.where(keep, pltpu.roll(tile, 16 * j, 1) if j else tile, low)
            high = jnp.where(keep, pltpu.roll(tile, (16 * j + 16) % 128, 1) if j < 7 else tile, high)
        plow[q] = low
        phigh[q] = high

    x_copies = launch(
        [(plow, xr, (0, 0, -1)), (phigh, xl, (0, 0, 1))],
        halo_send, halo_recv, len(early) + len(late),
    )
    n_far = more_z * cy * 128

    def overlapped(values, table):
        m = lax.dot_general(
            values, table, (((1,), (1,)), ((), ())), preferred_element_type=F32
        )
        m = m[:cols] + m[cols:]
        return m + pltpu.roll(m, 256 - 8, 1)

    w_rows = stack.at[WW * 32 : WW * 32 + 32]
    for dz, tile in enumerate(
        (overlapped(w_rows[...], bnear[...]), overlapped(w_rows[:, :n_far], bfar[...]))
    ):
        for dy in range(2):
            upper, lower = tile[:8, dy * 128 : dy * 128 + 128], tile[8:, dy * 128 : dy * 128 + 128]
            parts4[dz, dy] = jnp.where(lane8 % 16 < 8, upper, pltpu.roll(lower, 8, 1))

    def span(step):
        return (max(0, -step), 2 - abs(step))

    slot_of = {}
    filled = 0
    for where in around:
        count = span(where[0])[1] * span(where[1])[1]
        slot_of[where] = filled
        filled += count
    part_copies = []
    for where in around:
        (z0, zn), (y0, yn) = span(where[0]), span(where[1])
        for z in range(z0, z0 + zn):
            at = slot_of[where] + (z - z0) * yn
            pltpu.make_async_remote_copy(
                src_ref=parts4.at[z, pl.ds(y0, yn)],
                dst_ref=parts_in.at[pl.ds(at, yn)],
                send_sem=part_sem.at[0],
                recv_sem=part_sem.at[1],
                device_id=neighbour(*where),
                device_id_type=MESH,
            ).start()
    late_copies = launch(late, halo_send, halo_recv, len(early))
    w_row = products(WW, HP, WW)
    w_row2 = products(WW, XX, HW)
    red1_ref[...] = finish(reduction)
    for copy in x_copies:
        copy.wait()
    for cell in range(own):
        left, right = xl[cell // 8], xr[cell // 8]
        turn = (112 - 16 * (cell % 8)) % 128
        left = pltpu.roll(left, turn, 1) if turn else left
        shift = (128 - 16 * (cell % 8)) % 128
        right = pltpu.roll(right, shift, 1) if shift else right
        edges[cell] = jnp.where(lane < 64, right, left)

    @pl.loop(0, cz)
    def _(z):
        for y in range(cy):
            cell = z * cy + y
            edge = edges[cell]
            centre = inner[cz + z, y]
            vv = v_ref[z, y : y + 1, :]
            total = centre * (vv - 1.5 * LAP_CENTER)
            for k, weight in enumerate(LAP_COEFFS, start=1):
                beside = pltpu.roll(jnp.where(lane < k, edge, centre), 128 - k, 1)
                beside = beside + pltpu.roll(jnp.where(lane >= 128 - k, edge, centre), k, 1)
                if k < cz:
                    beside = beside + (inner[cz + z + k, y] + inner[cz + z - k, y])
                for target in (y + k, y - k):
                    if 0 <= target < cy:
                        beside = beside + inner[cz + z, target]
                total = total - 0.5 * weight * beside
            hw_ref[cell] = total
    for sem in (part_sem.at[1], part_sem.at[0]):
        pltpu.make_async_copy(parts_in, parts_in, sem).wait()
    gathered = {}
    for dz in range(2):
        for dy in range(2):
            sums = {}
            for dx in (-1, 0, 1):
                total = None
                for from_z in range(2):
                    for from_y in range(2):
                        where = (dz - from_z, dy - from_y, dx)
                        if where == (0, 0, 0):
                            tile = parts4[dz, dy]
                        else:
                            (z0, _), (y0, yn) = span(where[0]), span(where[1])
                            tile = parts_in[slot_of[where] + (from_z - z0) * yn + from_y - y0]
                        total = tile if total is None else total + tile
                sums[dx] = total
            side = jnp.where(lane8 < 64, pltpu.roll(sums[-1], 64, 1), pltpu.roll(sums[1], 64, 1))
            gathered[dz, dy] = sums[0] + side
    lefts = []
    for dz in range(2):
        halves = []
        for dy in range(2):
            total = gathered[dz, dy]
            o = dz * 4 + dy * 2
            coefs = jnp.where(
                lane8 < 64, shared[o, pairs][:, :128], shared[o + 1, pairs][:, :128]
            )
            mixed = None
            for d in range(-nproj + 1, nproj):
                term = pltpu.roll(total, (128 - d) % 128, 1) if d else total
                term = term * coefs[d + nproj - 1 : d + nproj, :]
                mixed = term if mixed is None else mixed + term
            low_half = lane8 % 16 < 8
            mixed = jnp.concatenate(
                [
                    jnp.where(low_half, mixed, pltpu.roll(mixed, 8, 1)),
                    jnp.where(low_half, pltpu.roll(mixed, 120, 1), mixed),
                ],
                0,
            )
            high = mixed.astype(BF16)
            low = (mixed - high.astype(F32)).astype(BF16)
            halves.append(jnp.concatenate([high, low], 0))
        lefts.append(jnp.concatenate(halves, 1))

    def placed(left, table, z):
        m = lax.dot_general(
            left, table[:, z * cy * 128 : (z + 1) * cy * 128],
            (((1,), (0,)), ((), ())), preferred_element_type=F32,
        )
        return m[:cols] + m[cols:]

    for z in range(cz):
        total = placed(lefts[0], bnear, z)
        if z < more_z:
            total = total + placed(lefts[1], bfar, z)
        for y in range(cy):
            nf[z, y] = total[:, y * 128 : y * 128 + 128]
    for copy in copies + late_copies:
        copy.wait()
    for cell in range(own):
        z, y = cell // cy, cell % cy
        total = hw_ref[cell] + nf[z, y]
        weights = {}
        for k, weight in enumerate(LAP_COEFFS, start=1):
            keys = [("z", z + k), ("z", z - k), (1, y + k - cy), (1 if two_y else 0, y - k + cy)]
            for key, inside in zip(keys, (z + k < cz, z - k >= 0, y + k < cy, y - k >= 0)):
                if not inside:
                    weights[key] = weights.get(key, 0.0) - 0.5 * weight
        for (where, at), weight in weights.items():
            tile = zext[cz + at, y] if where == "z" else ybuf[where, z, at]
            total = total + weight * tile
        hw_ref[cell] = total
        split_store(HW, cell, total)
    outs[1].start()
    hw_row = products(HW, XX, HW + 1)
    second = jnp.where(lane < 96, hw_row, pltpu.roll(w_row2_pad(w_row2), 32, 1))
    sums2 = finish(reduced(1, paired(w_row, second)))
    weight = 1.0 / (own * cx * nz * ny * nx)
    sums1 = red1_ref[...]
    rows = jnp.concatenate([sums1, pltpu.roll(sums1, 112, 1), sums2, pltpu.roll(sums2, 112, 1)], 0)
    rows = rows * weight
    turned = jnp.transpose(jnp.concatenate([rows, jnp.zeros_like(rows)], 0))

    def direct(row, group, target):
        return rows[16 * row : 16 * row + 16, :], 32 * group, target

    def flipped(row, group, target):
        return turned[32 * group : 32 * group + 16, :], 16 * row, target

    def laid(parts):
        total = None
        for tile, begin, target in parts:
            shift = (16 * target - begin) % 128
            tile = pltpu.roll(tile, shift, 1) if shift else tile
            tile = jnp.where((lane >= 16 * target) & (lane < 16 * target + 16), tile, 0.0)
            total = tile if total is None else total + tile
        return total

    gram = [
        [direct(0, 2, 0), flipped(2, 2, 1), direct(0, 3, 2)],
        [direct(2, 2, 0), direct(3, 3, 1), direct(2, 3, 2)],
        [direct(1, 2, 0), flipped(2, 3, 1), direct(1, 3, 2)],
    ]
    rayleigh = [
        [flipped(0, 1, 0), flipped(3, 0, 1), direct(0, 0, 2)],
        [direct(2, 1, 0), flipped(3, 2, 1), direct(2, 0, 2)],
        [direct(1, 1, 0), flipped(3, 1, 1), direct(1, 0, 2)],
    ]
    for i in range(3):
        gram_ref[16 * i : 16 * i + 16, :] = laid(gram[i])[:, :48]
        ray_ref[16 * i : 16 * i + 16, :] = laid(rayleigh[i])[:, :48]
    for out in outs[2:]:
        out.start()
    for out in outs:
        out.wait()


def put_out(*refs):
    sems = refs[-1]
    half = len(refs) // 2
    copies = [
        pltpu.make_async_copy(source, target, sems.at[i])
        for i, (source, target) in enumerate(zip(refs[:half], refs[half : 2 * half]))
    ]
    for copy in copies:
        copy.start()
    for copy in copies:
        copy.wait()


def w_row2_pad(row):
    return jnp.concatenate([row, jnp.zeros((row.shape[0], 128 - row.shape[1]), row.dtype)], 1)


def per_device(
    sizes,
    block_x, block_hx, block_p, block_hp, potential, projectors, coupling,
    atom_count, proj_count, offsets, extents,
):
    cols, cz, cy, cx = block_x.shape
    slots, nproj = projectors.shape[-3], projectors.shape[-2]
    nz, ny, nx = sizes
    own = cz * cy
    turned = [
        jnp.transpose(b, (1, 2, 0, 3)).reshape(own, cols, cx)
        for b in (block_x, block_hx, block_p, block_hp)
    ]
    groups = (("gz", "gy"), ("gx",)) if nz * ny <= 16 else (("gz",), ("gy",), ("gx",))
    size_of = dict(zip(AXES, sizes))
    totals = []
    for group in groups:
        total = 1
        for a in group:
            total *= size_of[a]
        totals.append(total)
    tile = (cols, 128)
    rows = slots * nproj
    near, far = own * 128, (BZ - 1) * cy * 128
    scratch = [
        pltpu.VMEM((cols, 128), F32),
        pltpu.VMEM((own,) + tile, F32),
        pltpu.VMEM((own,) + tile, F32),
        pltpu.VMEM((3 * cols, 3 * cols), F32),
        pltpu.VMEM((3 * cols, 3 * cols), F32),
        pltpu.VMEM((cols, cols, 128), F32),
        pltpu.VMEM((nproj, nproj, slots), F32),
        pltpu.VMEM(potential.shape, F32),
        pltpu.VMEM(projectors.shape[3:], F32),
        pltpu.VMEM((192, own * 128), BF16),
        pltpu.VMEM((3 * cz, cy) + tile, F32),
        pltpu.VMEM((2, cz, cy) + tile, F32),
        pltpu.VMEM((tiles_of(own),) + tile, F32),
        pltpu.VMEM((tiles_of(own),) + tile, F32),
        pltpu.VMEM((tiles_of(own),) + tile, F32),
        pltpu.VMEM((tiles_of(own),) + tile, F32),
        pltpu.VMEM((own,) + tile, F32),
        pltpu.VMEM((3 * cz, cy) + tile, F32),
        pltpu.VMEM((cz, cy) + tile, F32),
        pltpu.VMEM((8, rows // 8 + 1, 8, BZ * BY * BX), F32),
        pltpu.SMEM((7,) + offsets.shape, jnp.int32),
        pltpu.VMEM((slots * BZ * (BY + cy - 1) + BY + 3 * (cy - 1), 8, 128), F32),
        pltpu.VMEM((256, near), BF16),
        pltpu.VMEM((256, far), BF16),
        pltpu.VMEM((2, 2, 8, 128), F32),
        pltpu.VMEM((44, 8, 128), F32),
    ]
    scratch += [pltpu.VMEM((t, cols, 128), F32) for t in totals] * 2
    scratch += [pltpu.VMEM((t, 8, 128), F32) for t in totals]
    scratch += [
        pltpu.SemaphoreType.DMA((3 * len(groups),)),
        pltpu.SemaphoreType.DMA((3 * len(groups),)),
        pltpu.SemaphoreType.DMA((10,)),
        pltpu.SemaphoreType.DMA((10,)),
        pltpu.SemaphoreType.DMA((14,)),
        pltpu.SemaphoreType.DMA((14,)),
        pltpu.SemaphoreType.DMA((2,)),
        pltpu.SemaphoreType.DMA((7,)),
        pltpu.SemaphoreType.DMA((4,)),
    ]
    scratch += [pltpu.VMEM((own,) + tile, F32)] * 4
    vmem = pl.BlockSpec(memory_space=pltpu.VMEM)
    smem = pl.BlockSpec(memory_space=pltpu.SMEM)
    w, hw, gram, rayleigh = pl.pallas_call(
        functools.partial(kernel, sizes, groups, (cz, cy, cx, slots, nproj, cols)),
        out_shape=(
            pltpu.VMEM((own,) + tile, F32),
            pltpu.VMEM((own,) + tile, F32),
            pltpu.VMEM((3 * cols, 3 * cols), F32),
            pltpu.VMEM((3 * cols, 3 * cols), F32),
        ),
        in_specs=[smem] * 4 + [pl.BlockSpec(memory_space=pltpu.HBM)] * 7,
        out_specs=(pl.BlockSpec(memory_space=pl.ANY),) * 4,
        scratch_shapes=scratch,
        compiler_params=pltpu.CompilerParams(
            collective_id=0, has_side_effects=True, vmem_limit_bytes=VMEM_LIMIT
        ),
    )(
        offsets, extents, atom_count, proj_count[0, 0],
        jnp.transpose(coupling[0, 0, 0], (1, 2, 0)),
        *turned, potential, projectors[0, 0, 0],
    )
    w, hw, gram, rayleigh = pl.pallas_call(
        put_out,
        out_shape=tuple(jax.ShapeDtypeStruct(b.shape, F32) for b in (w, hw, gram, rayleigh)),
        in_specs=[vmem] * 4,
        out_specs=(pl.BlockSpec(memory_space=pl.ANY),) * 4,
        scratch_shapes=[pltpu.SemaphoreType.DMA((4,))],
        compiler_params=pltpu.CompilerParams(vmem_limit_bytes=4 << 20),
    )(w, hw, gram, rayleigh)
    w, hw = (jnp.transpose(b.reshape(cz, cy, cols, cx), (2, 0, 1, 3)) for b in (w, hw))
    return (w, hw, gram, rayleigh)


def solution(mesh):
    sizes = tuple(mesh.shape[a] for a in AXES)
    in_specs = (
        P(None, "gz", "gy", "gx"),
        P(None, "gz", "gy", "gx"),
        P(None, "gz", "gy", "gx"),
        P(None, "gz", "gy", "gx"),
        P("gz", "gy", "gx"),
        P("gz", "gy", "gx", None, None, None),
        P("gz", "gy", "gx", None, None, None),
        P("gz", "gy", "gx"),
        P("gz", "gy", "gx", None),
        P(None, "gz", "gy", "gx", None),
        P(None, "gz", "gy", "gx", None),
    )
    out_specs = (P(None, "gz", "gy", "gx"), P(None, "gz", "gy", "gx"), P(), P())
    return jax.shard_map(
        functools.partial(per_device, sizes),
        mesh=mesh, in_specs=in_specs, out_specs=out_specs, check_vma=False,
    )
```

time: 44.9 us -> 37 us (0.82)
  Pallas kernels: 43.4 us -> 35.5 us
    pallas_call x1, Pallas kernels: 42.6 us -> 34.7 us  [per_device(): pl.pallas_call(functools.partial(kernel, sizes, groups, (cz, cy, cx, slot...]
where the time goes in v2:
time: 37 us; the launch traced here: 36.8 us
  Pallas kernels  35.5 us (96%)
  between operations  1.29 us (3%)
    pallas_call x1, Pallas kernels, per_device(): pl.pallas_call(functools.partial(kernel, sizes, groups, (cz, cy, cx, slot...  34.7 us
    pallas_call x1, Pallas kernels, per_device(): pl.pallas_call(put_out, out_shape=tuple((jax.ShapeDtypeStruct(b.shape, F3...  0.85 us

profile of v2, /device:TPU:0, one launch (start us, length us, event | category | flops | bytes accessed | tf_op | source)
XLA Modules:
  0.0 36.8 jit_solution(14666874993389476136)
XLA Ops:
  1.3 34.7 %shard_map.138 = (f32[36,16,128]{2,1,0:T(8,128)S(1)}, f32[36,16,128]{2,1,0:T(8,128)S(1)}, f32[48,48]{1,0:T(8,128)S(1)}, f32[48,48]{1,0:T(8,128)S(1)}) custom-call(s32[3,1,1,1,8]{4,3,2,1,0:T(1,128)} %off_ref.1, s32[3,1,1,1,8]{4,3,2,1,0:T(1,128)} %ext_ref.1, s32[1,1,1]{2,1,0:T(1,128)S(6)} %copy.15.count_ref, s32[1,8]{1,0:T(1,128)} %bitcast.29, ...), custom_call_target="tpu_custom_call" | custom-call | tf_op jit(solution)/shard_map/pallas_call | solution.py:726
  36.0 0.9 %shard_map.139 = (f32[36,16,128]{2,1,0:T(8,128)}, f32[36,16,128]{2,1,0:T(8,128)}, f32[48,48]{1,0:T(8,128)}, f32[48,48]{1,0:T(8,128)}) custom-call(f32[36,16,128]{2,1,0:T(8,128)S(1)} %get-tuple-element.12.refs_0_, f32[36,16,128]{2,1,0:T(8,128)S(1)} %get-tuple-element.13.refs_1_, f32[48,48]{1,0:T(8,128)S(1)} %get-tuple-element.14.refs_2_, ...), custom_call_target="tpu_custom_call" | custom-call | tf_op jit(solution)/shard_map/pallas_call | solution.py:745

commit v3 on v2

--- a/solution.py
+++ b/solution.py
@@ -78,9 +78,9 @@
 
 def kernel(
     sizes, groups, dims,
-    off_ref, ext_ref, count_ref, proj_ref, d_in, x_in, hx_in, p_in, hp_in, v_in, beta_in,
-    w_out, hw_out, gram_out, ray_out, red1_ref, w_ref, hw_ref, gram_ref, ray_ref,
-    acol, d_ref, v_ref, beta_ref,
+    off_in, ext_in, count_in, proj_in, d_in, x_in, hx_in, p_in, hp_in, v_in, beta_in,
+    w_out, hw_out, sums_out, red1_ref, w_ref, hw_ref, sums_ref,
+    off_ref, ext_ref, count_ref, proj_ref, acol, d_ref, v_ref, beta_ref,
     stack, zext, ybuf, plow, phigh, xr, xl, edges, inner, nf,
     shared, offs, lines, bnear, bfar, parts4, parts_in,
     *rest,
@@ -91,11 +91,13 @@
     bufs = (rest[:n_red], rest[n_red : 2 * n_red], rest[2 * n_red : 3 * n_red])
     rest = rest[3 * n_red :]
     red_send, red_recv, halo_send, halo_recv, atom_send, atom_recv, part_sem = rest[:7]
-    load_sem, out_sem, x_ref, hx_ref, p_ref, hp_ref = rest[7:]
+    load_sem, out_sem, xh, p_ref, hp_ref, raw, raw_v, raw_send, raw_recv = rest[7:]
+    x_ref, hx_ref = xh.at[0], xh.at[1]
     loads = []
     for i, (source, target) in enumerate(
         (
-            (x_in, x_ref), (hx_in, hx_ref), (v_in, v_ref), (beta_in, beta_ref),
+            (x_in, x_ref), (hx_in, hx_ref), (off_in, off_ref), (ext_in, ext_ref),
+            (count_in, count_ref), (proj_in, proj_ref), (v_in, v_ref), (beta_in, beta_ref),
             (p_in, p_ref), (hp_in, hp_ref), (d_in, d_ref),
         )
     ):
@@ -228,6 +230,7 @@
         load.wait()
     rows = slots * nproj
     pairs = rows // 8
+    columns = BZ * BY * BX // 128
     box_lane = lax.broadcasted_iota(jnp.int32, (nproj, BZ * BY * BX), 1)
     box_row = lax.broadcasted_iota(jnp.int32, (nproj, BZ * BY * BX), 0)
     box_a, box_b, box_c = box_lane // (BY * BX), box_lane // BX % BY, box_lane % BX
@@ -240,7 +243,10 @@
             & (box_c < ext_ref[2, 0, 0, 0, s])
         )
         at = s * nproj
-        shared[0, at // 8, at % 8 : at % 8 + nproj, :] = jnp.where(inside, beta_ref[s], 0.0)
+        kept = jnp.where(inside, beta_ref[s], 0.0)
+        for c in range(columns):
+            where = (0, at // 8 * columns + c, slice(at % 8, at % 8 + nproj), slice(None))
+            shared[where] = kept[:, c * 128 : c * 128 + 128]
     lane1 = lax.broadcasted_iota(jnp.int32, (1, 128), 1)
     lane16 = lax.broadcasted_iota(jnp.int32, (nproj, 128), 1)
     slot_at = lane16 % 64 // 16 * (8 // nproj) + lane16 % 8 // nproj
@@ -257,7 +263,7 @@
         row = jnp.zeros((1, 128), F32)
         for p in range(max(0, -d), min(nproj, nproj - d)):
             row = jnp.where(lane1 % nproj == p, table[p][p + d : p + d + 1, :], row)
-        shared[0, pairs, d + nproj - 1 : d + nproj, 0:128] = row
+        shared[0, pairs * columns, d + nproj - 1 : d + nproj, :] = row
     atom_copies = {}
     for o in (4, 2, 1, 6, 5, 3, 7):
         atom_copies[o] = [
@@ -307,7 +313,7 @@
         dz, dy, dx = octant[o]
 
         def expand(pair):
-            tiles = shared[o, pair]
+            tiles = [shared[o, pair * columns + c] for c in range(columns)]
             for half in range(8 // nproj):
                 s = pair * (8 // nproj) + half
                 ox = offset(2, s)
@@ -317,8 +323,7 @@
                 for k in range(in_tile):
                     shift = (ox + 128 - BX * k) & 127
                     for at in range(k, BZ * BY, in_tile):
-                        part = tiles[:, at // in_tile * 128 : at // in_tile * 128 + 128]
-                        part = jnp.where(keep, pltpu.roll(part, shift, 1), 0.0)
+                        part = jnp.where(keep, pltpu.roll(tiles[at // in_tile], shift, 1), 0.0)
                         lines[ahead + (s * BZ + at // BY) * width + at % BY] = part
 
         def offset(axis, s):
@@ -362,6 +367,27 @@
     build(0)
     next(solving)
     next(reduction)
+    early_z = cz // 3
+    early_to = [(-1, 0, 0), (1, 0, 0), (0, -1, 0)] + ([] if ny == 2 else [(0, 1, 0)])
+    raw_copies = []
+    for d, where in enumerate(early_to):
+        for i, (source, target) in enumerate(
+            (
+                (xh.at[:, pl.ds(0, early_z * cy)], raw.at[d]),
+                (v_ref.at[pl.ds(0, early_z)], raw_v.at[d]),
+            )
+        ):
+            raw_copies.append(
+                pltpu.make_async_remote_copy(
+                    src_ref=source,
+                    dst_ref=target,
+                    send_sem=raw_send.at[2 * d + i],
+                    recv_sem=raw_recv.at[2 * d + i],
+                    device_id=neighbour(*where),
+                    device_id_type=MESH,
+                )
+            )
+            raw_copies[-1].start()
     for o in (4, 1, 2, 5, 6, 3, 7):
         for copy in atom_copies[o]:
             copy.wait()
@@ -387,7 +413,7 @@
             split_store(WW, cell, value)
 
     two_y = ny == 2
-    split = cz // 2
+    split = early_z + (cz - early_z) // 2
 
     def some(ref, z, dz, y, dy):
         return ref.at[pl.ds(z, dz), pl.ds(y, dy)]
@@ -405,7 +431,7 @@
             sends.append(layers(ybuf.at[0], 0, z, dz, (0, 1, 0)))
         return sends
 
-    early = bulk(0, split)
+    early = bulk(early_z, split - early_z)
     late = bulk(split, cz - split)
 
     def launch(sends, send_sem, recv_sem, first=0):
@@ -428,7 +454,7 @@
     outs = [
         pltpu.make_async_copy(source, target, out_sem.at[i])
         for i, (source, target) in enumerate(
-            ((w_ref, w_out), (hw_ref, hw_out), (gram_ref, gram_out), (ray_ref, ray_out))
+            ((w_ref, w_out), (hw_ref, hw_out), (sums_ref, sums_out))
         )
     ]
     outs[0].start()
@@ -456,13 +482,17 @@
         m = m[:cols] + m[cols:]
         return m + pltpu.roll(m, 256 - 8, 1)
 
+    lane4 = lax.broadcasted_iota(jnp.int32, (4, 128), 1)
     w_rows = stack.at[WW * 32 : WW * 32 + 32]
     for dz, tile in enumerate(
         (overlapped(w_rows[...], bnear[...]), overlapped(w_rows[:, :n_far], bfar[...]))
     ):
         for dy in range(2):
             upper, lower = tile[:8, dy * 128 : dy * 128 + 128], tile[8:, dy * 128 : dy * 128 + 128]
-            parts4[dz, dy] = jnp.where(lane8 % 16 < 8, upper, pltpu.roll(lower, 8, 1))
+            both = jnp.where(lane8 % 16 < 8, upper, pltpu.roll(lower, 8, 1))
+            moved = pltpu.roll(both, 64, 1)
+            parts4[dz, dy, 0] = jnp.where(lane4 < 64, both[:4], moved[4:])
+            parts4[dz, dy, 1] = jnp.where(lane4 < 64, moved[:4], both[4:])
 
     def span(step):
         return (max(0, -step), 2 - abs(step))
@@ -470,26 +500,41 @@
     slot_of = {}
     filled = 0
     for where in around:
-        count = span(where[0])[1] * span(where[1])[1]
         slot_of[where] = filled
-        filled += count
-    part_copies = []
+        filled += span(where[0])[1] * span(where[1])[1] * span(where[2])[1]
     for where in around:
-        (z0, zn), (y0, yn) = span(where[0]), span(where[1])
+        (z0, zn), (y0, yn), (x0, xn) = (span(step) for step in where)
         for z in range(z0, z0 + zn):
-            at = slot_of[where] + (z - z0) * yn
-            pltpu.make_async_remote_copy(
-                src_ref=parts4.at[z, pl.ds(y0, yn)],
-                dst_ref=parts_in.at[pl.ds(at, yn)],
-                send_sem=part_sem.at[0],
-                recv_sem=part_sem.at[1],
-                device_id=neighbour(*where),
-                device_id_type=MESH,
-            ).start()
+            for y in range(y0, y0 + yn):
+                at = slot_of[where] + ((z - z0) * yn + y - y0) * xn
+                pltpu.make_async_remote_copy(
+                    src_ref=parts4.at[z, y, pl.ds(x0, xn)],
+                    dst_ref=parts_in.at[pl.ds(at, xn)],
+                    send_sem=part_sem.at[0],
+                    recv_sem=part_sem.at[1],
+                    device_id=neighbour(*where),
+                    device_id_type=MESH,
+                ).start()
     late_copies = launch(late, halo_send, halo_recv, len(early))
     w_row = products(WW, HP, WW)
     w_row2 = products(WW, XX, HW)
     red1_ref[...] = finish(reduction)
+    for copy in raw_copies:
+        copy.wait()
+    for d in range(len(early_to)):
+        target, base = ((zext, 2 * cz), (zext, 0), (ybuf.at[1], 0), (ybuf.at[0], 0))[d]
+
+        @pl.loop(0, early_z)
+        def _(z):
+            for y in range(cy):
+                cell = z * cy + y
+                xs = raw[d, 0, cell]
+                value = raw[d, 1, cell]
+                for k in range(cols):
+                    value = value - theta_cols[k] * xs[k : k + 1, :]
+                vv = raw_v[d, z, y : y + 1, :]
+                target[base + z, y] = value * (1.0 / (1.0 + vv * vv))
+
     for copy in x_copies:
         copy.wait()
     for cell in range(own):
@@ -523,21 +568,29 @@
     gathered = {}
     for dz in range(2):
         for dy in range(2):
-            sums = {}
-            for dx in (-1, 0, 1):
+            sums = []
+            for dx in range(2):
                 total = None
                 for from_z in range(2):
                     for from_y in range(2):
-                        where = (dz - from_z, dy - from_y, dx)
-                        if where == (0, 0, 0):
-                            tile = parts4[dz, dy]
-                        else:
-                            (z0, _), (y0, yn) = span(where[0]), span(where[1])
-                            tile = parts_in[slot_of[where] + (from_z - z0) * yn + from_y - y0]
-                        total = tile if total is None else total + tile
-                sums[dx] = total
-            side = jnp.where(lane8 < 64, pltpu.roll(sums[-1], 64, 1), pltpu.roll(sums[1], 64, 1))
-            gathered[dz, dy] = sums[0] + side
+                        for from_x in range(2):
+                            where = (dz - from_z, dy - from_y, dx - from_x)
+                            if where == (0, 0, 0):
+                                tile = parts4[dz, dy, dx]
+                            else:
+                                (z0, _), (y0, yn), (x0, xn) = (span(step) for step in where)
+                                at = ((from_z - z0) * yn + from_y - y0) * xn + from_x - x0
+                                tile = parts_in[slot_of[where] + at]
+                            total = tile if total is None else total + tile
+                sums.append(total)
+            turned = [pltpu.roll(total, 64, 1) for total in sums]
+            gathered[dz, dy] = jnp.concatenate(
+                [
+                    jnp.where(lane4 < 64, sums[0], turned[1]),
+                    jnp.where(lane4 < 64, turned[0], sums[1]),
+                ],
+                0,
+            )
     lefts = []
     for dz in range(2):
         halves = []
@@ -545,7 +598,7 @@
             total = gathered[dz, dy]
             o = dz * 4 + dy * 2
             coefs = jnp.where(
-                lane8 < 64, shared[o, pairs][:, :128], shared[o + 1, pairs][:, :128]
+                lane8 < 64, shared[o, pairs * columns], shared[o + 1, pairs * columns]
             )
             mixed = None
             for d in range(-nproj + 1, nproj):
@@ -580,6 +633,7 @@
             nf[z, y] = total[:, y * 128 : y * 128 + 128]
     for copy in copies + late_copies:
         copy.wait()
+    hw_sum = None
     for cell in range(own):
         z, y = cell // cy, cell % cy
         total = hw_ref[cell] + nf[z, y]
@@ -594,12 +648,34 @@
             total = total + weight * tile
         hw_ref[cell] = total
         split_store(HW, cell, total)
+        if y == cy - 1:
+            plane = slice(z * cy * 128, (z + 1) * cy * 128)
+            part = lax.dot_general(
+                stack[HW * 32 : HW * 32 + 32, plane], stack[XX * 32 : HW * 32, plane],
+                (((1,), (1,)), ((), ())), preferred_element_type=F32,
+            )
+            hw_sum = part if hw_sum is None else hw_sum + part
     outs[1].start()
-    hw_row = products(HW, XX, HW + 1)
+    hw_row = w_row2_pad(hw_sum[:cols] + hw_sum[cols:])
     second = jnp.where(lane < 96, hw_row, pltpu.roll(w_row2_pad(w_row2), 32, 1))
     sums2 = finish(reduced(1, paired(w_row, second)))
-    weight = 1.0 / (own * cx * nz * ny * nx)
-    sums1 = red1_ref[...]
+    sums_ref[...] = jnp.concatenate([red1_ref[...], sums2], 0)
+    outs[2].start()
+    for out in outs:
+        out.wait()
+
+
+def finish_out(weight, w_ref, hw_ref, sums_ref, w_out, hw_out, gram_out, ray_out, gram_ref, ray_ref, sems):
+    copies = [
+        pltpu.make_async_copy(source, target, sems.at[i])
+        for i, (source, target) in enumerate(
+            ((w_ref, w_out), (hw_ref, hw_out), (gram_ref, gram_out), (ray_ref, ray_out))
+        )
+    ]
+    for copy in copies[:2]:
+        copy.start()
+    sums1, sums2 = sums_ref[:16], sums_ref[16:]
+    lane = lax.broadcasted_iota(jnp.int32, (16, 128), 1)
     rows = jnp.concatenate([sums1, pltpu.roll(sums1, 112, 1), sums2, pltpu.roll(sums2, 112, 1)], 0)
     rows = rows * weight
     turned = jnp.transpose(jnp.concatenate([rows, jnp.zeros_like(rows)], 0))
@@ -632,20 +708,7 @@
     for i in range(3):
         gram_ref[16 * i : 16 * i + 16, :] = laid(gram[i])[:, :48]
         ray_ref[16 * i : 16 * i + 16, :] = laid(rayleigh[i])[:, :48]
-    for out in outs[2:]:
-        out.start()
-    for out in outs:
-        out.wait()
-
-
-def put_out(*refs):
-    sems = refs[-1]
-    half = len(refs) // 2
-    copies = [
-        pltpu.make_async_copy(source, target, sems.at[i])
-        for i, (source, target) in enumerate(zip(refs[:half], refs[half : 2 * half]))
-    ]
-    for copy in copies:
+    for copy in copies[2:]:
         copy.start()
     for copy in copies:
         copy.wait()
@@ -683,8 +746,11 @@
         pltpu.VMEM((cols, 128), F32),
         pltpu.VMEM((own,) + tile, F32),
         pltpu.VMEM((own,) + tile, F32),
-        pltpu.VMEM((3 * cols, 3 * cols), F32),
-        pltpu.VMEM((3 * cols, 3 * cols), F32),
+        pltpu.VMEM((2 * cols, 128), F32),
+        pltpu.SMEM(offsets.shape, jnp.int32),
+        pltpu.SMEM(extents.shape, jnp.int32),
+        pltpu.SMEM(atom_count.shape, jnp.int32),
+        pltpu.SMEM(proj_count.shape[2:], jnp.int32),
         pltpu.VMEM((cols, cols, 128), F32),
         pltpu.VMEM((nproj, nproj, slots), F32),
         pltpu.VMEM(potential.shape, F32),
@@ -699,13 +765,13 @@
         pltpu.VMEM((own,) + tile, F32),
         pltpu.VMEM((3 * cz, cy) + tile, F32),
         pltpu.VMEM((cz, cy) + tile, F32),
-        pltpu.VMEM((8, rows // 8 + 1, 8, BZ * BY * BX), F32),
+        pltpu.VMEM((8, rows // 8 * (BZ * BY * BX // 128) + 1, 8, 128), F32),
         pltpu.SMEM((7,) + offsets.shape, jnp.int32),
         pltpu.VMEM((slots * BZ * (BY + cy - 1) + BY + 3 * (cy - 1), 8, 128), F32),
         pltpu.VMEM((256, near), BF16),
         pltpu.VMEM((256, far), BF16),
-        pltpu.VMEM((2, 2, 8, 128), F32),
-        pltpu.VMEM((44, 8, 128), F32),
+        pltpu.VMEM((2, 2, 2, 4, 128), F32),
+        pltpu.VMEM((56, 4, 128), F32),
     ]
     scratch += [pltpu.VMEM((t, cols, 128), F32) for t in totals] * 2
     scratch += [pltpu.VMEM((t, 8, 128), F32) for t in totals]
@@ -717,22 +783,30 @@
         pltpu.SemaphoreType.DMA((14,)),
         pltpu.SemaphoreType.DMA((14,)),
         pltpu.SemaphoreType.DMA((2,)),
-        pltpu.SemaphoreType.DMA((7,)),
-        pltpu.SemaphoreType.DMA((4,)),
-    ]
-    scratch += [pltpu.VMEM((own,) + tile, F32)] * 4
+        pltpu.SemaphoreType.DMA((11,)),
+        pltpu.SemaphoreType.DMA((3,)),
+    ]
+    ways = 3 if ny == 2 else 4
+    early_z = cz // 3
+    scratch += [
+        pltpu.VMEM((2, own) + tile, F32),
+        pltpu.VMEM((own,) + tile, F32),
+        pltpu.VMEM((own,) + tile, F32),
+        pltpu.VMEM((ways, 2, early_z * cy) + tile, F32),
+        pltpu.VMEM((ways, early_z, cy, 128), F32),
+        pltpu.SemaphoreType.DMA((2 * ways,)),
+        pltpu.SemaphoreType.DMA((2 * ways,)),
+    ]
     vmem = pl.BlockSpec(memory_space=pltpu.VMEM)
-    smem = pl.BlockSpec(memory_space=pltpu.SMEM)
-    w, hw, gram, rayleigh = pl.pallas_call(
+    w, hw, sums = pl.pallas_call(
         functools.partial(kernel, sizes, groups, (cz, cy, cx, slots, nproj, cols)),
         out_shape=(
             pltpu.VMEM((own,) + tile, F32),
             pltpu.VMEM((own,) + tile, F32),
-            pltpu.VMEM((3 * cols, 3 * cols), F32),
-            pltpu.VMEM((3 * cols, 3 * cols), F32),
+            pltpu.VMEM((2 * cols, 128), F32),
         ),
-        in_specs=[smem] * 4 + [pl.BlockSpec(memory_space=pltpu.HBM)] * 7,
-        out_specs=(pl.BlockSpec(memory_space=pl.ANY),) * 4,
+        in_specs=[pl.BlockSpec(memory_space=pltpu.HBM)] * 11,
+        out_specs=(pl.BlockSpec(memory_space=pl.ANY),) * 3,
         scratch_shapes=scratch,
         compiler_params=pltpu.CompilerParams(
             collective_id=0, has_side_effects=True, vmem_limit_bytes=VMEM_LIMIT
@@ -742,14 +816,20 @@
         jnp.transpose(coupling[0, 0, 0], (1, 2, 0)),
         *turned, potential, projectors[0, 0, 0],
     )
+    square = jax.ShapeDtypeStruct((3 * cols, 3 * cols), F32)
+    field = jax.ShapeDtypeStruct((own,) + tile, F32)
     w, hw, gram, rayleigh = pl.pallas_call(
-        put_out,
-        out_shape=tuple(jax.ShapeDtypeStruct(b.shape, F32) for b in (w, hw, gram, rayleigh)),
-        in_specs=[vmem] * 4,
+        functools.partial(finish_out, 1.0 / (own * cx * nz * ny * nx)),
+        out_shape=(field, field, square, square),
+        in_specs=[vmem] * 3,
         out_specs=(pl.BlockSpec(memory_space=pl.ANY),) * 4,
-        scratch_shapes=[pltpu.SemaphoreType.DMA((4,))],
+        scratch_shapes=[
+            pltpu.VMEM(square.shape, F32),
+            pltpu.VMEM(square.shape, F32),
+            pltpu.SemaphoreType.DMA((4,)),
+        ],
         compiler_params=pltpu.CompilerParams(vmem_limit_bytes=4 << 20),
-    )(w, hw, gram, rayleigh)
+    )(w, hw, sums)
     w, hw = (jnp.transpose(b.reshape(cz, cy, cols, cx), (2, 0, 1, 3)) for b in (w, hw))
     return (w, hw, gram, rayleigh)
 

time: 37 us -> 33.3 us (0.90)
  Pallas kernels: 35.5 us -> 31.9 us
    pallas_call x1, Pallas kernels: 34.7 us -> 31 us  [per_device(): pl.pallas_call(functools.partial(kernel, sizes, groups, (cz, cy, cx, slot...]
where the time goes in v3:
time: 33.3 us; the launch traced here: 33.2 us
  Pallas kernels  31.9 us (96%)
  between operations  1.29 us (4%)
    pallas_call x1, Pallas kernels, per_device(): pl.pallas_call(functools.partial(kernel, sizes, groups, (cz, cy, cx, slot...  31 us
    pallas_call x1, Pallas kernels, per_device(): pl.pallas_call(functools.partial(finish_out, 1.0 / (own * cx * nz * ny *...  0.88 us

profile of v3, /device:TPU:0, one launch (start us, length us, event | category | flops | bytes accessed | tf_op | source)
XLA Modules:
  0.0 33.2 jit_solution(2975477639120311611)
XLA Ops:
  1.3 31.0 %shard_map.138 = (f32[36,16,128]{2,1,0:T(8,128)S(1)}, f32[36,16,128]{2,1,0:T(8,128)S(1)}, f32[32,128]{1,0:T(8,128)S(1)}) custom-call(s32[3,1,1,1,8]{4,3,2,1,0:T(1,128)} %off_in.1, s32[3,1,1,1,8]{4,3,2,1,0:T(1,128)} %ext_in.1, s32[1,1,1]{2,1,0:T(1,128)S(6)} %copy.15.count_in, s32[1,8]{1,0:T(1,128)} %bitcast.29, f32[4,4,8]{2,1,0:T(4,128)} %bitcast.28, ...), custom_call_target="tpu_custom_call" | custom-call | tf_op jit(solution)/shard_map/pallas_call | solution.py:801
  32.3 0.9 %shard_map.139 = (f32[36,16,128]{2,1,0:T(8,128)}, f32[36,16,128]{2,1,0:T(8,128)}, f32[48,48]{1,0:T(8,128)}, f32[48,48]{1,0:T(8,128)}) custom-call(f32[36,16,128]{2,1,0:T(8,128)S(1)} %get-tuple-element.11.w_ref, f32[36,16,128]{2,1,0:T(8,128)S(1)} %get-tuple-element.12.hw_ref, f32[32,128]{1,0:T(8,128)S(1)} %get-tuple-element.13.sums_ref), custom_call_target="tpu_custom_call" | custom-call | tf_op jit(solution)/shard_map/pallas_call | solution.py:821

commit v4 on v3

--- a/solution.py
+++ b/solution.py
@@ -18,8 +18,12 @@
 HP, HX, XX, PP, WW, HW = range(6)
 
 
+EDGE = 8
+PER_TILE = 128 // EDGE
+
+
 def tiles_of(count):
-    return -(-count // 8)
+    return -(-count // PER_TILE)
 
 
 def solved(packed, cols, acol):
@@ -79,19 +83,21 @@
 def kernel(
     sizes, groups, dims,
     off_in, ext_in, count_in, proj_in, d_in, x_in, hx_in, p_in, hp_in, v_in, beta_in,
-    w_out, hw_out, sums_out, red1_ref, w_ref, hw_ref, sums_ref,
+    w_out, hw_out, sums_out, w_ref, hw_ref, sums_ref,
     off_ref, ext_ref, count_ref, proj_ref, acol, d_ref, v_ref, beta_ref,
-    stack, zext, ybuf, plow, phigh, xr, xl, edges, inner, nf,
-    shared, offs, lines, bnear, bfar, parts4, parts_in,
+    stack, zext, ybuf, xr, xl, edge_out, edge_in, edge_v, edge_v_in, edges, inner, nf,
+    shared, trim, offs, lines, near0, near1, far0, far1, wside, parts4, parts_in,
     *rest,
 ):
     cz, cy, cx, slots, nproj, cols = dims
     nz, ny, nx = sizes
     n_red = len(groups)
-    bufs = (rest[:n_red], rest[n_red : 2 * n_red], rest[2 * n_red : 3 * n_red])
-    rest = rest[3 * n_red :]
+    slow = (("gx",), ("gz",), ("gy",))
+    n_slow = len(slow)
+    bufs = (rest[:n_slow], rest[n_slow : n_slow + n_red], rest[n_slow + n_red : n_slow + 2 * n_red])
+    rest = rest[n_slow + 2 * n_red :]
     red_send, red_recv, halo_send, halo_recv, atom_send, atom_recv, part_sem = rest[:7]
-    load_sem, out_sem, xh, p_ref, hp_ref, raw, raw_v, raw_send, raw_recv = rest[7:]
+    load_sem, out_sem, xh, p_ref, hp_ref, raw, raw_v, raw_send, raw_recv, edge_send, edge_recv = rest[7:]
     x_ref, hx_ref = xh.at[0], xh.at[1]
     loads = []
     for i, (source, target) in enumerate(
@@ -177,10 +183,11 @@
         return parts if count > 1 else parts[0]
 
     def reduced(which, payload):
-        for phase, group in enumerate(groups):
+        for phase, group in enumerate(slow if which == 0 else groups):
             buf = bufs[which][phase]
             _, index, total = member(group, 0)
-            send_sem, recv_sem = (sem.at[which * n_red + phase] for sem in (red_send, red_recv))
+            at = phase + (which and len(slow) + (which - 1) * n_red)
+            send_sem, recv_sem = red_send.at[at], red_recv.at[at]
             buf[index] = payload
             if phase == 0 and which == 2:
                 pl.semaphore_wait(barrier, greeted)
@@ -228,6 +235,7 @@
     next(solving)
     for load in loads[2:]:
         load.wait()
+    lane8 = lax.broadcasted_iota(jnp.int32, (8, 128), 1)
     rows = slots * nproj
     pairs = rows // 8
     columns = BZ * BY * BX // 128
@@ -264,6 +272,21 @@
         for p in range(max(0, -d), min(nproj, nproj - d)):
             row = jnp.where(lane1 % nproj == p, table[p][p + d : p + d + 1, :], row)
         shared[0, pairs * columns, d + nproj - 1 : d + nproj, :] = row
+    for pair in range(0, pairs, 2):
+        lasts = []
+        for p in (pair, pair + 1):
+            first, last = shared[0, p * columns], shared[0, p * columns + 1]
+            lasts.append(last)
+            trim[p] = jnp.where(
+                lane8 < 48, pltpu.roll(first, 112, 1),
+                jnp.where(lane8 < 96, pltpu.roll(first, 96, 1), pltpu.roll(last, 80, 1)),
+            )
+        trim[pairs + pair // 2] = jnp.where(
+            lane8 < 64,
+            jnp.where(lane8 < 16, pltpu.roll(lasts[0], 80, 1), pltpu.roll(lasts[0], 64, 1)),
+            jnp.where(lane8 < 80, pltpu.roll(lasts[1], 16, 1), lasts[1]),
+        )
+    trim[pairs + pairs // 2] = shared[0, pairs * columns]
     atom_copies = {}
     for o in (4, 2, 1, 6, 5, 3, 7):
         atom_copies[o] = [
@@ -276,7 +299,11 @@
                 device_id_type=MESH,
             )
             for i, (source, target) in enumerate(
-                ((off_ref, offs.at[o - 1]), (shared.at[0], shared.at[o]))
+                (
+                    (off_ref, offs.at[o - 1]),
+                    (trim, shared.at[o, pl.ds(0, pairs + pairs // 2 + 1)])
+                    if octant[o][1] else (shared.at[0], shared.at[o]),
+                )
             )
         ]
         for copy in atom_copies[o]:
@@ -292,13 +319,12 @@
 
     reduction = reduced(0, paired(first, p_row))
 
-    lane8 = lax.broadcasted_iota(jnp.int32, (8, 128), 1)
     row8 = lax.broadcasted_iota(jnp.int32, (8, 128), 0)
     in_tile = 128 // BX
     width = BY + cy - 1
     ahead = cy - 1
     nothing = ahead + slots * BZ * width + ahead
-    blank = jnp.zeros((16, 128), BF16)
+    tables = {(0, 0): near0, (0, 1): near1, (1, 0): far0, (1, 1): far1}
     blank_line = jnp.zeros((8, 128), F32)
 
     @pl.loop(0, slots * BZ)
@@ -313,18 +339,29 @@
         dz, dy, dx = octant[o]
 
         def expand(pair):
-            tiles = [shared[o, pair * columns + c] for c in range(columns)]
+            if dy:
+                tiles = [shared[o, pair], shared[o, pairs + pair // 2]]
+            else:
+                tiles = [shared[o, pair * columns + c] for c in range(columns)]
+            places = {}
+            for at in range(BZ * BY):
+                a, b = at // BY, at % BY
+                if not dy:
+                    places[at] = at // in_tile, at % in_tile
+                elif b and a * (BY - 1) + b - 1 < in_tile:
+                    places[at] = 0, a * (BY - 1) + b - 1
+                elif b:
+                    places[at] = 1, pair % 2 * (in_tile // 2) + a * (BY - 1) + b - 1 - in_tile
             for half in range(8 // nproj):
                 s = pair * (8 // nproj) + half
                 ox = offset(2, s)
                 along = (lane8 - ox + 128) & 127
                 side = lane8 < ox if dx else lane8 >= ox
                 keep = (along < BX) & side & (row8 // nproj == half)
-                for k in range(in_tile):
+                for at, (tile, k) in places.items():
                     shift = (ox + 128 - BX * k) & 127
-                    for at in range(k, BZ * BY, in_tile):
-                        part = jnp.where(keep, pltpu.roll(tiles[at // in_tile], shift, 1), 0.0)
-                        lines[ahead + (s * BZ + at // BY) * width + at % BY] = part
+                    part = jnp.where(keep, pltpu.roll(tiles[tile], shift, 1), 0.0)
+                    lines[ahead + (s * BZ + at // BY) * width + at % BY] = part
 
         def offset(axis, s):
             return off_ref[axis, 0, 0, 0, s] if o == 0 else offs[o - 1, axis, 0, 0, 0, s]
@@ -332,8 +369,8 @@
         for pair in range(pairs):
             expand(pair)
 
-        target = bfar if dz else bnear
-        top = o % 4 * 64
+        target = tables[dz, dy]
+        top = dx * 64
         ys = more_y if dy else cy
 
         @pl.loop(0, more_z if dz else cz)
@@ -344,13 +381,10 @@
                 ok = (a >= 0) & (a < BZ)
                 start = jnp.where(ok, ahead + (s * BZ + a) * width - offset(1, s), nothing - offset(1, s))
                 starts.append(start)
-            for y in range(cy):
-                column = pl.ds(pl.multiple_of((z * cy + y) * 128, 128), 128)
+            for y in range(ys):
+                column = pl.ds(pl.multiple_of((z * ys + y) * 128, 128), 128)
                 for pair in range(pairs):
                     at = top + pair * 16
-                    if y >= ys:
-                        target[at : at + 16, column] = blank
-                        continue
                     total = None
                     for half in range(8 // nproj):
                         start = starts[pair * (8 // nproj) + half] + (y + dy * cy)
@@ -364,9 +398,13 @@
         for y in range(cy):
             inner[z, y] = jnp.zeros((cols, 128), F32)
             inner[2 * cz + z, y] = jnp.zeros((cols, 128), F32)
+    def build_all(owners):
+        for o in owners:
+            for copy in atom_copies[o]:
+                copy.wait()
+            build(o)
+
     build(0)
-    next(solving)
-    next(reduction)
     early_z = cz // 3
     early_to = [(-1, 0, 0), (1, 0, 0), (0, -1, 0)] + ([] if ny == 2 else [(0, 1, 0)])
     raw_copies = []
@@ -388,12 +426,47 @@
                 )
             )
             raw_copies[-1].start()
-    for o in (4, 1, 2, 5, 6, 3, 7):
-        for copy in atom_copies[o]:
-            copy.wait()
-        build(o)
+    def packed(read, rows_of):
+        at_lane = lax.broadcasted_iota(jnp.int32, (rows_of, 128), 1)
+        for q in range(tiles_of(own)):
+            low = jnp.zeros((rows_of, 128), F32)
+            high = low
+            for j in range(min(PER_TILE, own - PER_TILE * q)):
+                tile = read(PER_TILE * q + j)
+                keep = (at_lane >= EDGE * j) & (at_lane < EDGE * j + EDGE)
+                low = jnp.where(keep, pltpu.roll(tile, EDGE * j, 1) if j else tile, low)
+                turn = (EDGE * j + EDGE) % 128
+                high = jnp.where(keep, pltpu.roll(tile, turn, 1) if turn else tile, high)
+            yield q, low, high
+
+    edge_v[...] = jnp.zeros(edge_v.shape, F32)
+    for kind in range(2):
+        for q, low, high in packed(lambda cell: xh[kind, cell], cols):
+            edge_out[0, kind, q] = low
+            edge_out[1, kind, q] = high
+    for q, low, high in packed(lambda cell: v_ref[cell // cy, cell % cy : cell % cy + 1, :], 1):
+        edge_v[0, q : q + 1, :] = low
+        edge_v[1, q : q + 1, :] = high
+    next(solving)
+    next(reduction)
+    edge_copies = []
+    for side, step in enumerate((-1, 1)):
+        for i, (source, target) in enumerate(
+            ((edge_out.at[side], edge_in.at[side]), (edge_v.at[side], edge_v_in.at[side]))
+        ):
+            edge_copies.append(
+                pltpu.make_async_remote_copy(
+                    src_ref=source,
+                    dst_ref=target,
+                    send_sem=edge_send.at[2 * side + i],
+                    recv_sem=edge_recv.at[2 * side + i],
+                    device_id=neighbour(0, 0, step),
+                    device_id_type=MESH,
+                )
+            )
+            edge_copies[-1].start()
+    build_all((4, 2, 6, 1, 5, 3, 7))
     sums0 = finish(solving)
-    next(reduction)
     sums0 = solved(sums0, cols, acol)
     theta_cols = sums0
 
@@ -411,6 +484,11 @@
             inner[cz + z, y] = value
             w_ref[cell] = value
             split_store(WW, cell, value)
+            if y < more_y:
+                place = pl.ds(pl.multiple_of((z * more_y + y) * 128, 128), 128)
+                high = value.astype(BF16)
+                low = (value - high.astype(F32)).astype(BF16)
+                wside[:, place] = jnp.concatenate([high, low], 0)
 
     two_y = ny == 2
     split = early_z + (cz - early_z) // 2
@@ -458,37 +536,21 @@
         )
     ]
     outs[0].start()
-    for q in range(tiles_of(own)):
-        low = jnp.zeros((cols, 128), F32)
-        high = low
-        for j in range(min(8, own - 8 * q)):
-            tile = zext[cz + (8 * q + j) // cy, (8 * q + j) % cy]
-            keep = (lane >= 16 * j) & (lane < 16 * j + 16)
-            low = jnp.where(keep, pltpu.roll(tile, 16 * j, 1) if j else tile, low)
-            high = jnp.where(keep, pltpu.roll(tile, (16 * j + 16) % 128, 1) if j < 7 else tile, high)
-        plow[q] = low
-        phigh[q] = high
-
-    x_copies = launch(
-        [(plow, xr, (0, 0, -1)), (phigh, xl, (0, 0, 1))],
-        halo_send, halo_recv, len(early) + len(late),
-    )
-    n_far = more_z * cy * 128
-
-    def overlapped(values, table):
-        m = lax.dot_general(
-            values, table, (((1,), (1,)), ((), ())), preferred_element_type=F32
-        )
-        m = m[:cols] + m[cols:]
-        return m + pltpu.roll(m, 256 - 8, 1)
-
+    w_rows = stack.at[WW * 32 : WW * 32 + 32]
     lane4 = lax.broadcasted_iota(jnp.int32, (4, 128), 1)
-    w_rows = stack.at[WW * 32 : WW * 32 + 32]
-    for dz, tile in enumerate(
-        (overlapped(w_rows[...], bnear[...]), overlapped(w_rows[:, :n_far], bfar[...]))
-    ):
+    for dz in range(2):
         for dy in range(2):
-            upper, lower = tile[:8, dy * 128 : dy * 128 + 128], tile[8:, dy * 128 : dy * 128 + 128]
+            table = tables[dz, dy]
+            source = wside if dy else w_rows
+            m = lax.dot_general(
+                table[...], source[:, : table.shape[1]],
+                (((1,), (1,)), ((), ())), preferred_element_type=F32,
+            )
+            m = jnp.concatenate([m, jnp.zeros((128, 128 - 2 * cols), F32)], 1)
+            m = jnp.transpose(m)
+            m = m[:cols] + m[cols : 2 * cols]
+            m = m + pltpu.roll(m, 128 - 8, 1)
+            upper, lower = m[:8], m[8:]
             both = jnp.where(lane8 % 16 < 8, upper, pltpu.roll(lower, 8, 1))
             moved = pltpu.roll(both, 64, 1)
             parts4[dz, dy, 0] = jnp.where(lane4 < 64, both[:4], moved[4:])
@@ -518,7 +580,16 @@
     late_copies = launch(late, halo_send, halo_recv, len(early))
     w_row = products(WW, HP, WW)
     w_row2 = products(WW, XX, HW)
-    red1_ref[...] = finish(reduction)
+    for copy in edge_copies:
+        copy.wait()
+    for side, target in enumerate((xr, xl)):
+        for q in range(tiles_of(own)):
+            value = edge_in[side, 1, q]
+            xs = edge_in[side, 0, q]
+            for k in range(cols):
+                value = value - theta_cols[k] * xs[k : k + 1, :]
+            vv = edge_v_in[side, q : q + 1, :]
+            target[q] = value * (1.0 / (1.0 + vv * vv))
     for copy in raw_copies:
         copy.wait()
     for d in range(len(early_to)):
@@ -535,13 +606,29 @@
                 vv = raw_v[d, z, y : y + 1, :]
                 target[base + z, y] = value * (1.0 / (1.0 + vv * vv))
 
-    for copy in x_copies:
-        copy.wait()
+    next(reduction)
+    @pl.loop(0, cz)
+    def _(z):
+        for y in range(cy):
+            centre = inner[cz + z, y]
+            vv = v_ref[z, y : y + 1, :]
+            total = centre * (vv - 1.5 * LAP_CENTER)
+            for k, weight in enumerate(LAP_COEFFS, start=1):
+                tiles = [inner[cz + z, t] for t in (y + k, y - k) if 0 <= t < cy]
+                if k < cz:
+                    tiles += [inner[cz + z + k, y], inner[cz + z - k, y]]
+                beside = None
+                for tile in tiles:
+                    beside = tile if beside is None else beside + tile
+                if beside is not None:
+                    total = total - 0.5 * weight * beside
+            hw_ref[z * cy + y] = total
+
     for cell in range(own):
-        left, right = xl[cell // 8], xr[cell // 8]
-        turn = (112 - 16 * (cell % 8)) % 128
+        left, right = xl[cell // PER_TILE], xr[cell // PER_TILE]
+        turn = (256 - EDGE - EDGE * (cell % PER_TILE)) % 128
         left = pltpu.roll(left, turn, 1) if turn else left
-        shift = (128 - 16 * (cell % 8)) % 128
+        shift = (128 - EDGE * (cell % PER_TILE)) % 128
         right = pltpu.roll(right, shift, 1) if shift else right
         edges[cell] = jnp.where(lane < 64, right, left)
 
@@ -551,16 +638,10 @@
             cell = z * cy + y
             edge = edges[cell]
             centre = inner[cz + z, y]
-            vv = v_ref[z, y : y + 1, :]
-            total = centre * (vv - 1.5 * LAP_CENTER)
+            total = hw_ref[cell]
             for k, weight in enumerate(LAP_COEFFS, start=1):
                 beside = pltpu.roll(jnp.where(lane < k, edge, centre), 128 - k, 1)
                 beside = beside + pltpu.roll(jnp.where(lane >= 128 - k, edge, centre), k, 1)
-                if k < cz:
-                    beside = beside + (inner[cz + z + k, y] + inner[cz + z - k, y])
-                for target in (y + k, y - k):
-                    if 0 <= target < cy:
-                        beside = beside + inner[cz + z, target]
                 total = total - 0.5 * weight * beside
             hw_ref[cell] = total
     for sem in (part_sem.at[1], part_sem.at[0]):
@@ -591,14 +672,14 @@
                 ],
                 0,
             )
-    lefts = []
+    coef_at = (pairs * columns, pairs + pairs // 2)
+    lefts = {}
     for dz in range(2):
-        halves = []
         for dy in range(2):
             total = gathered[dz, dy]
             o = dz * 4 + dy * 2
             coefs = jnp.where(
-                lane8 < 64, shared[o, pairs * columns], shared[o + 1, pairs * columns]
+                lane8 < 64, shared[o, coef_at[dy]], shared[o + 1, coef_at[dy]]
             )
             mixed = None
             for d in range(-nproj + 1, nproj):
@@ -615,22 +696,24 @@
             )
             high = mixed.astype(BF16)
             low = (mixed - high.astype(F32)).astype(BF16)
-            halves.append(jnp.concatenate([high, low], 0))
-        lefts.append(jnp.concatenate(halves, 1))
-
-    def placed(left, table, z):
-        m = lax.dot_general(
-            left, table[:, z * cy * 128 : (z + 1) * cy * 128],
-            (((1,), (0,)), ((), ())), preferred_element_type=F32,
-        )
-        return m[:cols] + m[cols:]
+            lefts[dz, dy] = jnp.concatenate([high, low], 0)
 
     for z in range(cz):
-        total = placed(lefts[0], bnear, z)
-        if z < more_z:
-            total = total + placed(lefts[1], bfar, z)
+        sums = {}
+        for dz in range(2 if z < more_z else 1):
+            for dy in range(2):
+                ys = more_y if dy else cy
+                m = lax.dot_general(
+                    lefts[dz, dy], tables[dz, dy][:, z * ys * 128 : (z + 1) * ys * 128],
+                    (((1,), (0,)), ((), ())), preferred_element_type=F32,
+                )
+                m = m[:cols] + m[cols:]
+                for y in range(ys):
+                    part = m[:, y * 128 : y * 128 + 128]
+                    sums[y] = sums[y] + part if y in sums else part
         for y in range(cy):
-            nf[z, y] = total[:, y * 128 : y * 128 + 128]
+            nf[z, y] = sums[y]
+    next(reduction)
     for copy in copies + late_copies:
         copy.wait()
     hw_sum = None
@@ -658,8 +741,12 @@
     outs[1].start()
     hw_row = w_row2_pad(hw_sum[:cols] + hw_sum[cols:])
     second = jnp.where(lane < 96, hw_row, pltpu.roll(w_row2_pad(w_row2), 32, 1))
-    sums2 = finish(reduced(1, paired(w_row, second)))
-    sums_ref[...] = jnp.concatenate([red1_ref[...], sums2], 0)
+    closing = reduced(1, paired(w_row, second))
+    next(closing)
+    sums1 = next(reduction)
+    next(closing)
+    sums2 = finish(closing)
+    sums_ref[...] = jnp.concatenate([sums1, sums2], 0)
     outs[2].start()
     for out in outs:
         out.wait()
@@ -741,9 +828,7 @@
         totals.append(total)
     tile = (cols, 128)
     rows = slots * nproj
-    near, far = own * 128, (BZ - 1) * cy * 128
     scratch = [
-        pltpu.VMEM((cols, 128), F32),
         pltpu.VMEM((own,) + tile, F32),
         pltpu.VMEM((own,) + tile, F32),
         pltpu.VMEM((2 * cols, 128), F32),
@@ -760,26 +845,33 @@
         pltpu.VMEM((2, cz, cy) + tile, F32),
         pltpu.VMEM((tiles_of(own),) + tile, F32),
         pltpu.VMEM((tiles_of(own),) + tile, F32),
-        pltpu.VMEM((tiles_of(own),) + tile, F32),
-        pltpu.VMEM((tiles_of(own),) + tile, F32),
+        pltpu.VMEM((2, 2, tiles_of(own)) + tile, F32),
+        pltpu.VMEM((2, 2, tiles_of(own)) + tile, F32),
+        pltpu.VMEM((2, 8 * (-(-tiles_of(own) // 8)), 128), F32),
+        pltpu.VMEM((2, 8 * (-(-tiles_of(own) // 8)), 128), F32),
         pltpu.VMEM((own,) + tile, F32),
         pltpu.VMEM((3 * cz, cy) + tile, F32),
         pltpu.VMEM((cz, cy) + tile, F32),
         pltpu.VMEM((8, rows // 8 * (BZ * BY * BX // 128) + 1, 8, 128), F32),
+        pltpu.VMEM((rows // 8 + rows // 16 + 1, 8, 128), F32),
         pltpu.SMEM((7,) + offsets.shape, jnp.int32),
         pltpu.VMEM((slots * BZ * (BY + cy - 1) + BY + 3 * (cy - 1), 8, 128), F32),
-        pltpu.VMEM((256, near), BF16),
-        pltpu.VMEM((256, far), BF16),
+        pltpu.VMEM((128, own * 128), BF16),
+        pltpu.VMEM((128, cz * (BY - 1) * 128), BF16),
+        pltpu.VMEM((128, (BZ - 1) * cy * 128), BF16),
+        pltpu.VMEM((128, (BZ - 1) * (BY - 1) * 128), BF16),
+        pltpu.VMEM((2 * cols, cz * (BY - 1) * 128), BF16),
         pltpu.VMEM((2, 2, 2, 4, 128), F32),
         pltpu.VMEM((56, 4, 128), F32),
     ]
-    scratch += [pltpu.VMEM((t, cols, 128), F32) for t in totals] * 2
+    scratch += [pltpu.VMEM((size_of[a], cols, 128), F32) for a in ("gx", "gz", "gy")]
+    scratch += [pltpu.VMEM((t, cols, 128), F32) for t in totals]
     scratch += [pltpu.VMEM((t, 8, 128), F32) for t in totals]
     scratch += [
-        pltpu.SemaphoreType.DMA((3 * len(groups),)),
-        pltpu.SemaphoreType.DMA((3 * len(groups),)),
-        pltpu.SemaphoreType.DMA((10,)),
-        pltpu.SemaphoreType.DMA((10,)),
+        pltpu.SemaphoreType.DMA((3 + 2 * len(groups),)),
+        pltpu.SemaphoreType.DMA((3 + 2 * len(groups),)),
+        pltpu.SemaphoreType.DMA((8,)),
+        pltpu.SemaphoreType.DMA((8,)),
         pltpu.SemaphoreType.DMA((14,)),
         pltpu.SemaphoreType.DMA((14,)),
         pltpu.SemaphoreType.DMA((2,)),
@@ -796,6 +888,8 @@
         pltpu.VMEM((ways, early_z, cy, 128), F32),
         pltpu.SemaphoreType.DMA((2 * ways,)),
         pltpu.SemaphoreType.DMA((2 * ways,)),
+        pltpu.SemaphoreType.DMA((4,)),
+        pltpu.SemaphoreType.DMA((4,)),
     ]
     vmem = pl.BlockSpec(memory_space=pltpu.VMEM)
     w, hw, sums = pl.pallas_call(

time: 33.3 us -> 32.6 us (0.979)
  Pallas kernels: 31.9 us -> 31.1 us
    pallas_call x1, Pallas kernels: 31 us -> 30.2 us  [per_device(): pl.pallas_call(functools.partial(kernel, sizes, groups, (cz, cy, cx, slot...]
where the time goes in v4:
time: 32.6 us; the launch traced here: 32.4 us
  Pallas kernels  31.1 us (95%)
  between operations  1.29 us (4%)
    pallas_call x1, Pallas kernels, per_device(): pl.pallas_call(functools.partial(kernel, sizes, groups, (cz, cy, cx, slot...  30.2 us
    pallas_call x1, Pallas kernels, per_device(): pl.pallas_call(functools.partial(finish_out, 1.0 / (own * cx * nz * ny *...  0.88 us

profile of v4, /device:TPU:0, one launch (start us, length us, event | category | flops | bytes accessed | tf_op | source)
XLA Modules:
  0.0 32.4 jit_solution(7459666954938968099)
XLA Ops:
  1.3 30.2 %shard_map.138 = (f32[36,16,128]{2,1,0:T(8,128)S(1)}, f32[36,16,128]{2,1,0:T(8,128)S(1)}, f32[32,128]{1,0:T(8,128)S(1)}) custom-call(s32[3,1,1,1,8]{4,3,2,1,0:T(1,128)} %off_in.1, s32[3,1,1,1,8]{4,3,2,1,0:T(1,128)} %ext_in.1, s32[1,1,1]{2,1,0:T(1,128)S(6)} %copy.15.count_in, s32[1,8]{1,0:T(1,128)} %bitcast.29, f32[4,4,8]{2,1,0:T(4,128)} %bitcast.28, ...), custom_call_target="tpu_custom_call" | custom-call | tf_op jit(solution)/shard_map/pallas_call | solution.py:895
  31.5 0.9 %shard_map.139 = (f32[36,16,128]{2,1,0:T(8,128)}, f32[36,16,128]{2,1,0:T(8,128)}, f32[48,48]{1,0:T(8,128)}, f32[48,48]{1,0:T(8,128)}) custom-call(f32[36,16,128]{2,1,0:T(8,128)S(1)} %get-tuple-element.11.w_ref, f32[36,16,128]{2,1,0:T(8,128)S(1)} %get-tuple-element.12.hw_ref, f32[32,128]{1,0:T(8,128)S(1)} %get-tuple-element.13.sums_ref), custom_call_target="tpu_custom_call" | custom-call | tf_op jit(solution)/shard_map/pallas_call | solution.py:915

commit v5 on v4

--- a/solution.py
+++ b/solution.py
@@ -536,10 +536,32 @@
         )
     ]
     outs[0].start()
+    def span(step):
+        return (max(0, -step), 2 - abs(step))
+
+    slot_of = {}
+    filled = 0
+    for where in around:
+        slot_of[where] = filled
+        filled += span(where[0])[1] * span(where[1])[1] * span(where[2])[1]
+    def hand_out(z, y):
+        for where in around:
+            (z0, zn), (y0, yn), (x0, xn) = (span(step) for step in where)
+            if z0 <= z < z0 + zn and y0 <= y < y0 + yn:
+                at = slot_of[where] + ((z - z0) * yn + y - y0) * xn
+                pltpu.make_async_remote_copy(
+                    src_ref=parts4.at[z, y, pl.ds(x0, xn)],
+                    dst_ref=parts_in.at[pl.ds(at, xn)],
+                    send_sem=part_sem.at[0],
+                    recv_sem=part_sem.at[1],
+                    device_id=neighbour(*where),
+                    device_id_type=MESH,
+                ).start()
+
     w_rows = stack.at[WW * 32 : WW * 32 + 32]
     lane4 = lax.broadcasted_iota(jnp.int32, (4, 128), 1)
-    for dz in range(2):
-        for dy in range(2):
+    for early_tiles in (((1, 1), (1, 0), (0, 1)), ((0, 0),)):
+        for dz, dy in early_tiles:
             table = tables[dz, dy]
             source = wside if dy else w_rows
             m = lax.dot_general(
@@ -555,28 +577,9 @@
             moved = pltpu.roll(both, 64, 1)
             parts4[dz, dy, 0] = jnp.where(lane4 < 64, both[:4], moved[4:])
             parts4[dz, dy, 1] = jnp.where(lane4 < 64, moved[:4], both[4:])
-
-    def span(step):
-        return (max(0, -step), 2 - abs(step))
-
-    slot_of = {}
-    filled = 0
-    for where in around:
-        slot_of[where] = filled
-        filled += span(where[0])[1] * span(where[1])[1] * span(where[2])[1]
-    for where in around:
-        (z0, zn), (y0, yn), (x0, xn) = (span(step) for step in where)
-        for z in range(z0, z0 + zn):
-            for y in range(y0, y0 + yn):
-                at = slot_of[where] + ((z - z0) * yn + y - y0) * xn
-                pltpu.make_async_remote_copy(
-                    src_ref=parts4.at[z, y, pl.ds(x0, xn)],
-                    dst_ref=parts_in.at[pl.ds(at, xn)],
-                    send_sem=part_sem.at[0],
-                    recv_sem=part_sem.at[1],
-                    device_id=neighbour(*where),
-                    device_id_type=MESH,
-                ).start()
+        for dz, dy in early_tiles:
+            hand_out(dz, dy)
+
     late_copies = launch(late, halo_send, halo_recv, len(early))
     w_row = products(WW, HP, WW)
     w_row2 = products(WW, XX, HW)
@@ -606,7 +609,6 @@
                 vv = raw_v[d, z, y : y + 1, :]
                 target[base + z, y] = value * (1.0 / (1.0 + vv * vv))
 
-    next(reduction)
     @pl.loop(0, cz)
     def _(z):
         for y in range(cy):
@@ -644,6 +646,7 @@
                 beside = beside + pltpu.roll(jnp.where(lane >= 128 - k, edge, centre), k, 1)
                 total = total - 0.5 * weight * beside
             hw_ref[cell] = total
+    next(reduction)
     for sem in (part_sem.at[1], part_sem.at[0]):
         pltpu.make_async_copy(parts_in, parts_in, sem).wait()
     gathered = {}
@@ -713,7 +716,6 @@
                     sums[y] = sums[y] + part if y in sums else part
         for y in range(cy):
             nf[z, y] = sums[y]
-    next(reduction)
     for copy in copies + late_copies:
         copy.wait()
     hw_sum = None
@@ -743,8 +745,9 @@
     second = jnp.where(lane < 96, hw_row, pltpu.roll(w_row2_pad(w_row2), 32, 1))
     closing = reduced(1, paired(w_row, second))
     next(closing)
+    next(reduction)
+    next(closing)
     sums1 = next(reduction)
-    next(closing)
     sums2 = finish(closing)
     sums_ref[...] = jnp.concatenate([sums1, sums2], 0)
     outs[2].start()

time: 32.6 us -> 32.4 us (level)
  no operation moved by 1% of the time
where the time goes in v5:
time: 32.4 us; the launch traced here: 32.2 us
  Pallas kernels  30.9 us (95%)
  between operations  1.29 us (4%)
    pallas_call x1, Pallas kernels, per_device(): pl.pallas_call(functools.partial(kernel, sizes, groups, (cz, cy, cx, slot...  30 us
    pallas_call x1, Pallas kernels, per_device(): pl.pallas_call(functools.partial(finish_out, 1.0 / (own * cx * nz * ny *...  0.88 us

profile of v5, /device:TPU:0, one launch (start us, length us, event | category | flops | bytes accessed | tf_op | source)
XLA Modules:
  0.0 32.2 jit_solution(10114918096160848819)
XLA Ops:
  1.3 30.0 %shard_map.138 = (f32[36,16,128]{2,1,0:T(8,128)S(1)}, f32[36,16,128]{2,1,0:T(8,128)S(1)}, f32[32,128]{1,0:T(8,128)S(1)}) custom-call(s32[3,1,1,1,8]{4,3,2,1,0:T(1,128)} %off_in.1, s32[3,1,1,1,8]{4,3,2,1,0:T(1,128)} %ext_in.1, s32[1,1,1]{2,1,0:T(1,128)S(6)} %copy.15.count_in, s32[1,8]{1,0:T(1,128)} %bitcast.29, f32[4,4,8]{2,1,0:T(4,128)} %bitcast.28, ...), custom_call_target="tpu_custom_call" | custom-call | tf_op jit(solution)/shard_map/pallas_call | solution.py:898
  31.3 0.9 %shard_map.139 = (f32[36,16,128]{2,1,0:T(8,128)}, f32[36,16,128]{2,1,0:T(8,128)}, f32[48,48]{1,0:T(8,128)}, f32[48,48]{1,0:T(8,128)}) custom-call(f32[36,16,128]{2,1,0:T(8,128)S(1)} %get-tuple-element.11.w_ref, f32[36,16,128]{2,1,0:T(8,128)S(1)} %get-tuple-element.12.hw_ref, f32[32,128]{1,0:T(8,128)S(1)} %get-tuple-element.13.sums_ref), custom_call_target="tpu_custom_call" | custom-call | tf_op jit(solution)/shard_map/pallas_call | solution.py:918

commit v6 on v5

--- a/solution.py
+++ b/solution.py
@@ -465,7 +465,7 @@
                 )
             )
             edge_copies[-1].start()
-    build_all((4, 2, 6, 1, 5, 3, 7))
+    build_all((4, 2, 6, 1, 5, 3))
     sums0 = finish(solving)
     sums0 = solved(sums0, cols, acol)
     theta_cols = sums0
@@ -536,6 +536,7 @@
         )
     ]
     outs[0].start()
+    build_all((7,))
     def span(step):
         return (max(0, -step), 2 - abs(step))
 

time: 32.4 us -> 32.6 us (level)
  no operation moved by 1% of the time
where the time goes in v6:
time: 32.6 us; the launch traced here: 32.4 us
  Pallas kernels  31.1 us (95%)
  between operations  1.29 us (4%)
    pallas_call x1, Pallas kernels, per_device(): pl.pallas_call(functools.partial(kernel, sizes, groups, (cz, cy, cx, slot...  30.2 us
    pallas_call x1, Pallas kernels, per_device(): pl.pallas_call(functools.partial(finish_out, 1.0 / (own * cx * nz * ny *...  0.88 us

profile of v6, /device:TPU:0, one launch (start us, length us, event | category | flops | bytes accessed | tf_op | source)
XLA Modules:
  0.0 32.4 jit_solution(2038489312822020961)
XLA Ops:
  1.3 30.2 %shard_map.138 = (f32[36,16,128]{2,1,0:T(8,128)S(1)}, f32[36,16,128]{2,1,0:T(8,128)S(1)}, f32[32,128]{1,0:T(8,128)S(1)}) custom-call(s32[3,1,1,1,8]{4,3,2,1,0:T(1,128)} %off_in.1, s32[3,1,1,1,8]{4,3,2,1,0:T(1,128)} %ext_in.1, s32[1,1,1]{2,1,0:T(1,128)S(6)} %copy.15.count_in, s32[1,8]{1,0:T(1,128)} %bitcast.29, f32[4,4,8]{2,1,0:T(4,128)} %bitcast.28, ...), custom_call_target="tpu_custom_call" | custom-call | tf_op jit(solution)/shard_map/pallas_call | solution.py:899
  31.5 0.9 %shard_map.139 = (f32[36,16,128]{2,1,0:T(8,128)}, f32[36,16,128]{2,1,0:T(8,128)}, f32[48,48]{1,0:T(8,128)}, f32[48,48]{1,0:T(8,128)}) custom-call(f32[36,16,128]{2,1,0:T(8,128)S(1)} %get-tuple-element.11.w_ref, f32[36,16,128]{2,1,0:T(8,128)S(1)} %get-tuple-element.12.hw_ref, f32[32,128]{1,0:T(8,128)S(1)} %get-tuple-element.13.sums_ref), custom_call_target="tpu_custom_call" | custom-call | tf_op jit(solution)/shard_map/pallas_call | solution.py:919
